TPU v7x, 32 devices: a whole 2x2x4 slice. The times are simulated.
32 devices in a mesh: groups: 2 (over x), rows: 16 (over z, y, core).
Axes of the slice: x: 2, y: 2, z: 4, core: 2. Of those that a mesh axis runs over, the one named last changes fastest.
Arguments:
- bin_ids: int32 [16384, 512], P(('groups', 'rows')), parts along dimension 0, may hold values from 0 to 255
- gradients: bfloat16 [16384], P(('groups', 'rows')), parts along dimension 0, may hold values from -6 to 6
- hessians: bfloat16 [16384], P(('groups', 'rows')), parts along dimension 0, may hold values from 0.049804688 to 1
- node_ids: int32 [16384], P(('groups', 'rows')), parts along dimension 0, may hold values from 0 to 15
- predictions: float32 [16384], P(('groups', 'rows')), parts along dimension 0, may hold values from -6 to 6
- split_feature: int32 [32], P('groups'), parts along dimension 0, may hold values from 0 to 511
- split_bin: int32 [32], P('groups'), parts along dimension 0, may hold values from 0 to 254
Outputs:
- gains: float32 [1024, 16, 256], P(('groups', 'rows')), parts along dimension 0
- best_gain: float32 [32], P('groups'), parts along dimension 0
- leaf_values: float32 [2, 32], P(None, 'groups'), parts along dimension 1
- new_predictions: float32 [16384], P(('groups', 'rows')), parts along dimension 0
There are 2 independent parts, one for each index of `groups`. A program takes and returns all parts, laid end to end along the dimension named above; each array names one. Nothing has to cross between parts.
All inputs are finite; a program needn't handle non-finite values.
Results may differ from a plain program's by a relative error of at most 0.0003.
Values sent between devices are 32-bit elements; how exact they have to be, the bound alone decides.
No kernel may reach another device: no remote copies, remote signals or barrier semaphores. Data moves between devices by JAX's collectives and lax.ppermute only.
A program may use at most 64 MiB of HBM per device.

v0:
```python
import math

import jax
import jax.numpy as jnp
from jax import lax
from jax.sharding import PartitionSpec as P

F = 512
BINS = 256
NODES = 16


l2_penalty = 1.0
shrinkage = 0.5


def combined_all(part, axis, combine):
    gathered = jax.tree.map(lambda a: lax.all_gather(a, axis), part)

    def take(source):
        return jax.tree.map(lambda a: lax.dynamic_index_in_dim(a, source, 0, False), gathered)

    return lax.fori_loop(
        1, lax.axis_size(axis), lambda source, state: combine(state, take(source)), take(0)
    )


def node_weights(node_ids, gradients, hessians):
    node_hot = node_ids[:, None] == jnp.arange(NODES, dtype=jnp.int32)[None, :]
    zero_value = jnp.zeros((), jnp.bfloat16)
    grad_part = jnp.where(node_hot, gradients[:, None], zero_value)
    hess_part = jnp.where(node_hot, hessians[:, None], zero_value)
    return jnp.concatenate([grad_part, hess_part], axis=1)


def bin_onehot(columns):
    return (columns[:, :, None] == jnp.arange(BINS, dtype=jnp.int32)[None, None, :]).astype(
        jnp.bfloat16
    )


def combine_pair(earlier, later):
    return (jnp.maximum(earlier[0], later[0]), earlier[1] + later[1])


def body(bin_ids, gradients, hessians, node_ids, predictions, split_feature, split_bin):
    owned = F // lax.axis_size("rows")
    first_feature = lax.axis_index("rows") * owned
    weights = node_weights(node_ids, gradients, hessians)
    feat_block = math.gcd(F, 32)

    def one_block(block_index):
        columns = lax.dynamic_slice_in_dim(bin_ids, block_index * feat_block, feat_block, 1)
        return jnp.einsum(
            "rk,rfb->fkb", weights, bin_onehot(columns), preferred_element_type=jnp.float32
        )

    blocks = lax.map(one_block, jnp.arange(F // feat_block, dtype=jnp.int32))
    full_terms = blocks.reshape(F, 2 * NODES, BINS)
    histogram = lax.psum_scatter(full_terms, "rows", scatter_dimension=0, tiled=True)
    cum_grad = jnp.cumsum(histogram[:, :NODES], axis=2)
    cum_hess = jnp.cumsum(histogram[:, NODES:], axis=2)
    tot_grad = cum_grad[:, :, -1:]
    tot_hess = cum_hess[:, :, -1:]
    gains = 0.5 * (
        cum_grad**2 / (cum_hess + l2_penalty)
        + (tot_grad - cum_grad) ** 2 / (tot_hess - cum_hess + l2_penalty)
        - tot_grad**2 / (tot_hess + l2_penalty)
    )
    best_local = jnp.max(gains, axis=(0, 2))
    local_feature = split_feature - first_feature
    owner_sel = jnp.arange(owned, dtype=jnp.int32)[:, None] == local_feature[None, :]
    bin_sel = jnp.arange(BINS, dtype=jnp.int32)[None, :] == split_bin[:, None]
    picked = owner_sel[:, :, None] & bin_sel[None, :, :]
    left_grad = jnp.sum(jnp.where(picked, cum_grad, 0.0), axis=(0, 2))
    left_hess = jnp.sum(jnp.where(picked, cum_hess, 0.0), axis=(0, 2))
    node_grad = jnp.sum(jnp.where(owner_sel, tot_grad[:, :, 0], 0.0), axis=0)
    node_hess = jnp.sum(jnp.where(owner_sel, tot_hess[:, :, 0], 0.0), axis=0)
    leaf_local = jnp.stack([left_grad, left_hess, node_grad, node_hess])
    best_gain, leaf_stats = combined_all((best_local, leaf_local), "rows", combine_pair)
    leaf_left = -leaf_stats[0] / (leaf_stats[1] + l2_penalty)
    leaf_right = -(leaf_stats[2] - leaf_stats[0]) / (leaf_stats[3] - leaf_stats[1] + l2_penalty)
    leaf_values = jnp.stack([leaf_left, leaf_right])
    node_hot = node_ids[:, None] == jnp.arange(NODES, dtype=jnp.int32)[None, :]
    row_feature = jnp.sum(jnp.where(node_hot, split_feature[None, :], 0), axis=1)
    row_threshold = jnp.sum(jnp.where(node_hot, split_bin[None, :], 0), axis=1)
    row_bin = jnp.take_along_axis(bin_ids, row_feature[:, None], axis=1)[:, 0]
    left_row = jnp.sum(jnp.where(node_hot, leaf_left[None, :], 0.0), axis=1)
    right_row = jnp.sum(jnp.where(node_hot, leaf_right[None, :], 0.0), axis=1)
    new_predictions = predictions + shrinkage * jnp.where(
        row_bin > row_threshold, right_row, left_row
    )
    return (gains, best_gain, leaf_values, new_predictions)


def solution(mesh):
    return jax.shard_map(
        body,
        mesh=mesh,
        in_specs=(
            P(("groups", "rows"), None),
            P(("groups", "rows")),
            P(("groups", "rows")),
            P(("groups", "rows")),
            P(("groups", "rows")),
            P("groups"),
            P("groups"),
        ),
        out_specs=(
            P(("groups", "rows"), None, None),
            P("groups"),
            P(None, "groups"),
            P(("groups", "rows")),
        ),
        check_vma=False,
    )
```

profile of v0, /device:TPU:0, one launch (start us, length us, event | category | flops | bytes accessed | tf_op | source)
XLA Modules:
  0.0 398.6 jit_solution(5753148695925994905)
XLA Ops:
  7.2 1.6 copy.50
  8.8 0.7 fusion.8
  9.5 107.6 %while.27 = (s32[]{:T(128)}, f32[16,32,32,256]{3,2,1,0:T(8,128)}, s32[16]{0:T(128)S(1)}, s32[512,512]{0,1:T(8,128)S(1)}, bf16[512,32]{0,1:T(8,128)(2,1)S(1)}, /*...) while((s32[]{:T(128)}, f32[16,32,32,256]{3,2,1,0:T(8,128)}, s32[16]{0:T(128)S(1)}, ...), condition=%wide.region_1.2_spmd, body=%wide.region_0.1_spmd.sunk | while | flops 272629760 | bytes 1278619 | solution.py:58
  9.5 0.6 dynamic_slice.45
  10.8 5.5 %fusion.21 = f32[16,32,32,256]{3,2,1,0:T(8,128)} fusion(f32[16,32,32,256]{3,2,1,0:T(8,128)} %get-tuple-element.296, s32[]{:T(128)} %get-tuple-element.295, s32[512,32]{0,1:T(8,128)S(1)} %constant_dynamic-slice_fusion.2, bf16[512,32]{0,1:T(8,128)(2,1)S(1)} %get-tuple-element.308), kind=kOutput, calls=%fused_computation.5.clone.1 | convolution fusion | flops 272629760 | bytes 1147392 | tf_op jit(solution)/shard_map/while/body/eval_jaxpr/rk,rfb->fkb/dot_general | solution.py:54
  16.3 0.6 dynamic_slice.45
  17.5 5.5 %fusion.21 = f32[16,32,32,256]{3,2,1,0:T(8,128)} fusion(f32[16,32,32,256]{3,2,1,0:T(8,128)} %get-tuple-element.296, s32[]{:T(128)} %get-tuple-element.295, s32[512,32]{0,1:T(8,128)S(1)} %constant_dynamic-slice_fusion.2, bf16[512,32]{0,1:T(8,128)(2,1)S(1)} %get-tuple-element.308), kind=kOutput, calls=%fused_computation.5.clone.1 | convolution fusion | flops 272629760 | bytes 1147392 | tf_op jit(solution)/shard_map/while/body/eval_jaxpr/rk,rfb->fkb/dot_general | solution.py:54
  23.0 0.6 dynamic_slice.45
  24.2 5.5 %fusion.21 = f32[16,32,32,256]{3,2,1,0:T(8,128)} fusion(f32[16,32,32,256]{3,2,1,0:T(8,128)} %get-tuple-element.296, s32[]{:T(128)} %get-tuple-element.295, s32[512,32]{0,1:T(8,128)S(1)} %constant_dynamic-slice_fusion.2, bf16[512,32]{0,1:T(8,128)(2,1)S(1)} %get-tuple-element.308), kind=kOutput, calls=%fused_computation.5.clone.1 | convolution fusion | flops 272629760 | bytes 1147392 | tf_op jit(solution)/shard_map/while/body/eval_jaxpr/rk,rfb->fkb/dot_general | solution.py:54
  29.7 0.6 dynamic_slice.45
  31.0 5.5 %fusion.21 = f32[16,32,32,256]{3,2,1,0:T(8,128)} fusion(f32[16,32,32,256]{3,2,1,0:T(8,128)} %get-tuple-element.296, s32[]{:T(128)} %get-tuple-element.295, s32[512,32]{0,1:T(8,128)S(1)} %constant_dynamic-slice_fusion.2, bf16[512,32]{0,1:T(8,128)(2,1)S(1)} %get-tuple-element.308), kind=kOutput, calls=%fused_computation.5.clone.1 | convolution fusion | flops 272629760 | bytes 1147392 | tf_op jit(solution)/shard_map/while/body/eval_jaxpr/rk,rfb->fkb/dot_general | solution.py:54
  36.4 0.6 dynamic_slice.45
  37.7 5.5 %fusion.21 = f32[16,32,32,256]{3,2,1,0:T(8,128)} fusion(f32[16,32,32,256]{3,2,1,0:T(8,128)} %get-tuple-element.296, s32[]{:T(128)} %get-tuple-element.295, s32[512,32]{0,1:T(8,128)S(1)} %constant_dynamic-slice_fusion.2, bf16[512,32]{0,1:T(8,128)(2,1)S(1)} %get-tuple-element.308), kind=kOutput, calls=%fused_computation.5.clone.1 | convolution fusion | flops 272629760 | bytes 1147392 | tf_op jit(solution)/shard_map/while/body/eval_jaxpr/rk,rfb->fkb/dot_general | solution.py:54
  43.2 0.6 dynamic_slice.45
  44.4 5.5 %fusion.21 = f32[16,32,32,256]{3,2,1,0:T(8,128)} fusion(f32[16,32,32,256]{3,2,1,0:T(8,128)} %get-tuple-element.296, s32[]{:T(128)} %get-tuple-element.295, s32[512,32]{0,1:T(8,128)S(1)} %constant_dynamic-slice_fusion.2, bf16[512,32]{0,1:T(8,128)(2,1)S(1)} %get-tuple-element.308), kind=kOutput, calls=%fused_computation.5.clone.1 | convolution fusion | flops 272629760 | bytes 1147392 | tf_op jit(solution)/shard_map/while/body/eval_jaxpr/rk,rfb->fkb/dot_general | solution.py:54
  49.9 0.6 dynamic_slice.45
  51.1 5.5 %fusion.21 = f32[16,32,32,256]{3,2,1,0:T(8,128)} fusion(f32[16,32,32,256]{3,2,1,0:T(8,128)} %get-tuple-element.296, s32[]{:T(128)} %get-tuple-element.295, s32[512,32]{0,1:T(8,128)S(1)} %constant_dynamic-slice_fusion.2, bf16[512,32]{0,1:T(8,128)(2,1)S(1)} %get-tuple-element.308), kind=kOutput, calls=%fused_computation.5.clone.1 | convolution fusion | flops 272629760 | bytes 1147392 | tf_op jit(solution)/shard_map/while/body/eval_jaxpr/rk,rfb->fkb/dot_general | solution.py:54
  56.6 0.6 dynamic_slice.45
  57.9 5.5 %fusion.21 = f32[16,32,32,256]{3,2,1,0:T(8,128)} fusion(f32[16,32,32,256]{3,2,1,0:T(8,128)} %get-tuple-element.296, s32[]{:T(128)} %get-tuple-element.295, s32[512,32]{0,1:T(8,128)S(1)} %constant_dynamic-slice_fusion.2, bf16[512,32]{0,1:T(8,128)(2,1)S(1)} %get-tuple-element.308), kind=kOutput, calls=%fused_computation.5.clone.1 | convolution fusion | flops 272629760 | bytes 1147392 | tf_op jit(solution)/shard_map/while/body/eval_jaxpr/rk,rfb->fkb/dot_general | solution.py:54
  63.3 0.6 dynamic_slice.45
  64.6 5.5 %fusion.21 = f32[16,32,32,256]{3,2,1,0:T(8,128)} fusion(f32[16,32,32,256]{3,2,1,0:T(8,128)} %get-tuple-element.296, s32[]{:T(128)} %get-tuple-element.295, s32[512,32]{0,1:T(8,128)S(1)} %constant_dynamic-slice_fusion.2, bf16[512,32]{0,1:T(8,128)(2,1)S(1)} %get-tuple-element.308), kind=kOutput, calls=%fused_computation.5.clone.1 | convolution fusion | flops 272629760 | bytes 1147392 | tf_op jit(solution)/shard_map/while/body/eval_jaxpr/rk,rfb->fkb/dot_general | solution.py:54
  70.0 0.6 dynamic_slice.45
  71.3 5.5 %fusion.21 = f32[16,32,32,256]{3,2,1,0:T(8,128)} fusion(f32[16,32,32,256]{3,2,1,0:T(8,128)} %get-tuple-element.296, s32[]{:T(128)} %get-tuple-element.295, s32[512,32]{0,1:T(8,128)S(1)} %constant_dynamic-slice_fusion.2, bf16[512,32]{0,1:T(8,128)(2,1)S(1)} %get-tuple-element.308), kind=kOutput, calls=%fused_computation.5.clone.1 | convolution fusion | flops 272629760 | bytes 1147392 | tf_op jit(solution)/shard_map/while/body/eval_jaxpr/rk,rfb->fkb/dot_general | solution.py:54
  76.8 0.6 dynamic_slice.45
  78.0 5.5 %fusion.21 = f32[16,32,32,256]{3,2,1,0:T(8,128)} fusion(f32[16,32,32,256]{3,2,1,0:T(8,128)} %get-tuple-element.296, s32[]{:T(128)} %get-tuple-element.295, s32[512,32]{0,1:T(8,128)S(1)} %constant_dynamic-slice_fusion.2, bf16[512,32]{0,1:T(8,128)(2,1)S(1)} %get-tuple-element.308), kind=kOutput, calls=%fused_computation.5.clone.1 | convolution fusion | flops 272629760 | bytes 1147392 | tf_op jit(solution)/shard_map/while/body/eval_jaxpr/rk,rfb->fkb/dot_general | solution.py:54
  83.5 0.6 dynamic_slice.45
  84.7 5.5 %fusion.21 = f32[16,32,32,256]{3,2,1,0:T(8,128)} fusion(f32[16,32,32,256]{3,2,1,0:T(8,128)} %get-tuple-element.296, s32[]{:T(128)} %get-tuple-element.295, s32[512,32]{0,1:T(8,128)S(1)} %constant_dynamic-slice_fusion.2, bf16[512,32]{0,1:T(8,128)(2,1)S(1)} %get-tuple-element.308), kind=kOutput, calls=%fused_computation.5.clone.1 | convolution fusion | flops 272629760 | bytes 1147392 | tf_op jit(solution)/shard_map/while/body/eval_jaxpr/rk,rfb->fkb/dot_general | solution.py:54
  90.2 0.6 dynamic_slice.45
  91.5 5.5 %fusion.21 = f32[16,32,32,256]{3,2,1,0:T(8,128)} fusion(f32[16,32,32,256]{3,2,1,0:T(8,128)} %get-tuple-element.296, s32[]{:T(128)} %get-tuple-element.295, s32[512,32]{0,1:T(8,128)S(1)} %constant_dynamic-slice_fusion.2, bf16[512,32]{0,1:T(8,128)(2,1)S(1)} %get-tuple-element.308), kind=kOutput, calls=%fused_computation.5.clone.1 | convolution fusion | flops 272629760 | bytes 1147392 | tf_op jit(solution)/shard_map/while/body/eval_jaxpr/rk,rfb->fkb/dot_general | solution.py:54
  96.9 0.6 dynamic_slice.45
  98.2 5.5 %fusion.21 = f32[16,32,32,256]{3,2,1,0:T(8,128)} fusion(f32[16,32,32,256]{3,2,1,0:T(8,128)} %get-tuple-element.296, s32[]{:T(128)} %get-tuple-element.295, s32[512,32]{0,1:T(8,128)S(1)} %constant_dynamic-slice_fusion.2, bf16[512,32]{0,1:T(8,128)(2,1)S(1)} %get-tuple-element.308), kind=kOutput, calls=%fused_computation.5.clone.1 | convolution fusion | flops 272629760 | bytes 1147392 | tf_op jit(solution)/shard_map/while/body/eval_jaxpr/rk,rfb->fkb/dot_general | solution.py:54
  103.6 0.6 dynamic_slice.45
  104.9 5.5 %fusion.21 = f32[16,32,32,256]{3,2,1,0:T(8,128)} fusion(f32[16,32,32,256]{3,2,1,0:T(8,128)} %get-tuple-element.296, s32[]{:T(128)} %get-tuple-element.295, s32[512,32]{0,1:T(8,128)S(1)} %constant_dynamic-slice_fusion.2, bf16[512,32]{0,1:T(8,128)(2,1)S(1)} %get-tuple-element.308), kind=kOutput, calls=%fused_computation.5.clone.1 | convolution fusion | flops 272629760 | bytes 1147392 | tf_op jit(solution)/shard_map/while/body/eval_jaxpr/rk,rfb->fkb/dot_general | solution.py:54
  110.4 0.6 dynamic_slice.45
  111.6 5.5 %fusion.21 = f32[16,32,32,256]{3,2,1,0:T(8,128)} fusion(f32[16,32,32,256]{3,2,1,0:T(8,128)} %get-tuple-element.296, s32[]{:T(128)} %get-tuple-element.295, s32[512,32]{0,1:T(8,128)S(1)} %constant_dynamic-slice_fusion.2, bf16[512,32]{0,1:T(8,128)(2,1)S(1)} %get-tuple-element.308), kind=kOutput, calls=%fused_computation.5.clone.1 | convolution fusion | flops 272629760 | bytes 1147392 | tf_op jit(solution)/shard_map/while/body/eval_jaxpr/rk,rfb->fkb/dot_general | solution.py:54
  117.2 0.6 copy-done.5
  118.1 0.3 copy-done
  118.4 4.5 %gather_fusion = s32[512]{0:T(512)S(1)} fusion(s32[512,512]{1,0:T(8,128)S(1)} %copy-done, s32[512]{0:T(512)S(1)} %bitcast.82), kind=kCustom, calls=%fused_computation | custom fusion | bytes 8192 | tf_op jit(solution)/shard_map/jit(take_along_axis)/gather | solution.py:87
  122.9 0.6 dynamic-slice
  124.2 173.2 %reduce-scatter.2.cloned.1.call-done = f32[32,32,256]{2,1,0:T(8,128)} async-done(((f32[512,32,256]{2,1,0:T(8,128)}), f32[32,32,256]{2,1,0:T(8,128)}) %reduce-scatter.2.cloned.1.call-update) | async-done | bytes 1048592 | tf_op jit(solution)/shard_map/reduce_scatter | solution.py:60
  297.4 1.3 slice_bitcast_fusion.1
  298.8 18.1 %reduce-window.14 = f32[32,16,2,128]{3,1,2,0:T(8,128)S(1)} reduce-window(f32[32,16,2,128]{3,1,2,0:T(8,128)S(1)} %get-tuple-element.223, f32[]{:T(128)} %constant.92.clone.1), window={size=1x1x1x128 pad=0_0x0_0x0_0x127_0}, to_apply=%region_3.4 | reduce-window | flops 16646144 | bytes 1048580 | tf_op jit(solution)/shard_map/reduce-window
  316.9 0.2 slice.58
  317.1 0.4 copy.52
  317.6 0.2 copy_bitcast_fusion.1
  317.8 0.1 slice.63
  318.0 0.2 copy.68
  318.1 0.2 copy.70
  318.4 18.1 %reduce-window.16 = f32[32,16,2,128]{3,1,2,0:T(8,128)S(1)} reduce-window(f32[32,16,2,128]{3,1,2,0:T(8,128)S(1)} %get-tuple-element.222, f32[]{:T(128)} %constant.92.clone.1), window={size=1x1x1x128 pad=0_0x0_0x0_0x127_0}, to_apply=%region_5.6 | reduce-window | flops 16646144 | bytes 1048580 | tf_op jit(solution)/shard_map/reduce-window.2
  336.5 0.2 slice.61
  336.7 0.4 copy.56
  337.3 0.2 copy_bitcast_fusion
  337.5 0.1 slice.64
  337.6 0.2 copy.69
  337.8 0.2 copy.71
  338.1 0.2 fusion.14
  338.3 0.9 fusion.5
  339.2 0.2 dynamic-update-slice
  339.5 31.5 %all-reduce = f32[256]{0:T(256)S(1)} all-reduce(f32[256]{0:T(256)S(1)} %dynamic-update-slice), channel_id=2, replica_groups=mesh['groups'=2,'rows'=16] {'rows'}, use_global_device_ids=true, to_apply=%add | all-reduce | flops 256 | bytes 2048
  371.0 1.3 subtract_multiply_fusion
  372.4 17.2 %all-gather.2 = f32[16,4,16]{2,1,0:T(4,128)S(1)} all-gather(f32[1,4,16]{2,1,0:T(4,128)S(1)} %maximum_bitcast_fusion), channel_id=3, replica_groups=mesh['groups'=2,'rows'=16] {'rows'}, dimensions={0}, use_global_device_ids=true | all-gather | bytes 4352 | tf_op jit(solution)/shard_map/all_gather | solution.py:18
  389.6 0.8 while.28
  390.5 0.6 pad_maximum_fusion.1
  391.1 0.6 multiply_add_fusion
  (89 shorter events, 1.8 us)
Async XLA Ops:
  7.2 290.2 %reduce-scatter.2.cloned.1.call-start = ((), (), s32[]{:S(2)}) async-start(), calls=%async_computation.1 | async-start | bytes 17825792 | tf_op jit(solution)/shard_map/reduce_scatter | solution.py:60
  117.1 0.7 copy-start.5
  117.1 0.8 copy-start.1
  117.1 0.8 copy-start.4
  117.1 1.3 copy-start
  117.1 5.8 %copy-start.6 = (u32[32]{0:T(128)S(1)}, u32[32]{0:T(128)}, u32[]{:S(2)}) copy-start(u32[32]{0:T(128)} %constant.118) | copy-start | bytes 388
  117.1 274.0 %copy-start.3 = (f32[512]{0:T(512)S(1)}, f32[512]{0:T(512)}, u32[]{:S(2)}) copy-start(f32[512]{0:T(512)} %param.15) | copy-start | bytes 6148
  390.4 1.3 copy-start.2
Sparse Core Ops, SparseCore 0:
  117.3 180.0 reduce-scatter.1
where the time goes:
time: 399 us
  waiting for transfers between devices  173 us (43%)
  matrix products  87.4 us (22%)
  blocking collectives  48.7 us (12%)
  other arithmetic  42 us (11%)
  local copies, waits for them, and re-layouts  21.3 us (5%)
  between operations  14.9 us (4%)
  loops' own time  11 us (3%)
    reduce_scatter x1, waiting for transfers between devices, body(): lax.psum_scatter(full_terms, 'rows', scatter_dimension=0, tiled=True)  173 us
    dot_general x16, matrix products, one_block(): jnp.einsum('rk,rfb->fkb', weights, bin_onehot(columns), preferred_element...  87.4 us
    another operation x6, other arithmetic  36.8 us
    unnamed x1, blocking collectives  31.5 us
    all_gather x1, blocking collectives, combined_all(): gathered = jax.tree.map(lambda a: lax.all_gather(a, axis), part)  17.2 us
    another operation x1, loops' own time, body(): blocks = lax.map(one_block, jnp.arange(F // feat_block, dtype=jnp.int32))  10.6 us
    dynamic_slice x16, local copies, waits for them, and re-layouts, body(): blocks = lax.map(one_block, jnp.arange(F // feat_block, dtype=jnp.int32))  9.32 us
  transfers between devices with their start and end apart: 1, of which 1 were waited for; matrix products, arithmetic and copies ran while one was open for 1% of the time, Pallas kernels for 0%

commit v1 on v0

v1 whole, which is shorter than its diff:
```python
import functools

import jax
import jax.numpy as jnp
from jax import lax
from jax.experimental import pallas as pl
from jax.experimental.pallas import tpu as pltpu
from jax.sharding import PartitionSpec as P

BINS = 256
NODES = 16
LANES = 128
HALF = BINS // 2
EXTRA = 4

l2_penalty = 1.0
shrinkage = 0.5

VMEM = pl.BlockSpec(memory_space=pltpu.VMEM)


def prep_kernel(bins_ref, info_ref, node_ref, split_ref, pay_ref):
    peers, _, _ = pay_ref.shape
    rows, feats = bins_ref.shape
    owned = feats // peers
    chunks = rows // LANES
    node_col = lax.broadcasted_iota(jnp.int32, (NODES, LANES), 0)
    feat_pos = lax.broadcasted_iota(jnp.int32, (NODES, feats), 1)
    pick = jnp.where(feat_pos == split_ref[:, 0:1], 1.0, 0.0).astype(jnp.bfloat16)
    for c in range(chunks):
        block = bins_ref[c * LANES : (c + 1) * LANES, :].astype(jnp.float32)
        picked = lax.dot_general(
            pick,
            block.astype(jnp.bfloat16),
            (((1,), (1,)), ((), ())),
            preferred_element_type=jnp.float32,
        )
        member = node_ref[c : c + 1, :] == node_col
        right = picked > split_ref[:, 1:2].astype(jnp.float32)
        side = jnp.sum(jnp.where(member & right, 1.0, 0.0), axis=0, keepdims=True)
        flipped = block.T
        info = [info_ref[k, c : c + 1, :] for k in range(3)] + [side]
        for d in range(peers):
            pay_ref[d, c * owned : (c + 1) * owned, :] = flipped[d * owned : (d + 1) * owned, :]
            for k in range(EXTRA):
                at = chunks * owned + k * chunks + c
                pay_ref[d, at : at + 1, :] = info[k]


def hist_kernel(pay_ref, mine_ref, pred_ref, gains_ref, best_ref, leaf_ref, new_ref, w_ref):
    peers = pay_ref.shape[0]
    owned = gains_ref.shape[0]
    chunks = pred_ref.shape[0]
    base = chunks * owned
    bf16 = jnp.bfloat16
    node_col = lax.broadcasted_iota(jnp.int32, (NODES, LANES), 0).astype(jnp.float32)

    def build(s, sums):
        out = list(sums)
        for c in range(chunks):
            g, h, node, side = (
                pay_ref[s, base + k * chunks + c : base + k * chunks + c + 1, :]
                for k in range(EXTRA)
            )
            member = node == node_col
            wg = jnp.where(member, g, 0.0)
            wh = jnp.where(member, h, 0.0)
            w_ref[s, c] = jnp.concatenate([wg, wh], axis=0).astype(bf16)
            left = side < 0.5
            out[0] = out[0] + jnp.where(left, wg, 0.0)
            out[1] = out[1] + jnp.where(left, wh, 0.0)
            out[2] = out[2] + wg
            out[3] = out[3] + wh
        return tuple(out)

    zero = jnp.zeros((NODES, LANES), jnp.float32)
    sums = lax.fori_loop(0, peers, build, (zero,) * 4)
    left_grad, left_hess, node_grad, node_hess = (
        jnp.sum(x, axis=1, keepdims=True) for x in sums
    )
    leaf_left = -left_grad / (left_hess + l2_penalty)
    leaf_right = -(node_grad - left_grad) / (node_hess - left_hess + l2_penalty)
    lane = lax.broadcasted_iota(jnp.int32, (NODES, LANES), 1)
    both = jnp.where(lane == 0, leaf_left, leaf_right)
    both = jnp.concatenate([both, jnp.zeros((LANES - NODES, LANES), jnp.float32)], axis=0)
    leaf_ref[...] = both.T[0:2, 0:NODES]
    for c in range(chunks):
        node = mine_ref[2 * chunks + c : 2 * chunks + c + 1, :]
        side = mine_ref[3 * chunks + c : 3 * chunks + c + 1, :]
        value = jnp.where(side < 0.5, leaf_left, leaf_right)
        value = jnp.sum(jnp.where(node == node_col, value, 0.0), axis=0, keepdims=True)
        new_ref[c : c + 1, :] = pred_ref[c : c + 1, :] + shrinkage * value

    row16 = lax.broadcasted_iota(jnp.int32, (16, LANES), 0)
    steps = [(row16 + 16 * i).astype(jnp.float32).astype(bf16) for i in range(HALF // 16)]
    one = jnp.ones((16, LANES), bf16)
    nil = jnp.zeros((16, LANES), bf16)

    def terms(s, c, f):
        row = jnp.broadcast_to(pay_ref[s, pl.ds(c * owned + f, 1), :], (8, LANES))
        high = jnp.where(row >= HALF, 1.0, 0.0)
        low = row - HALF * high
        low16 = jnp.concatenate([low, low], axis=0).astype(bf16)
        high16 = jnp.concatenate([high, high], axis=0).astype(bf16)
        rhs = jnp.concatenate([jnp.where(low16 <= t, one, nil) for t in steps], axis=0)
        first = one - high16
        w = w_ref[s, c]
        wg, wh = w[:NODES], w[NODES:]
        lhs = jnp.concatenate([wg * first, wh * first, wg * high16, wh * high16], axis=0)
        return lhs, rhs

    unroll = min(peers, 8)

    def scan(acc):
        def quad(q, best):
            def sources(j, carry):
                for u in range(unroll):
                    s = j * unroll + u
                    for t in range(chunks // 2):
                        for m in range(2):
                            f = q * 4 + m * 2
                            part = [[terms(s, 2 * t + i, f + e) for i in range(2)] for e in range(2)]
                            lhs = jnp.concatenate(
                                [jnp.concatenate([p[0] for p in e], axis=1) for e in part], axis=0
                            )
                            rhs = jnp.concatenate(
                                [jnp.concatenate([p[1] for p in e], axis=1) for e in part], axis=0
                            )
                            reg = (u * (chunks // 2) + t) % 2
                            pltpu.matmul_push_rhs(
                                rhs, staging_register=reg, mxu_index=m, transpose=True
                            )
                            pltpu.matmul_acc_lhs(acc[m], lhs, load_staged_rhs=reg)
                return carry

            lax.fori_loop(0, peers // unroll, sources, 0)
            for m in range(2):
                out = pltpu.matmul_pop(acc[m])
                for e in range(2):
                    c = out[e * 64 : (e + 1) * 64, e * HALF : (e + 1) * HALF]
                    cums = []
                    for k in range(2):
                        a, b = c[k * 16 : (k + 1) * 16], c[32 + k * 16 : 48 + k * 16]
                        cums.append(jnp.concatenate([a, b + a[:, HALF - 1 : HALF]], axis=1))
                    cum_grad, cum_hess = cums
                    tot_grad = cum_grad[:, BINS - 1 : BINS]
                    tot_hess = cum_hess[:, BINS - 1 : BINS]
                    gain = 0.5 * (
                        cum_grad * cum_grad / (cum_hess + l2_penalty)
                        + (tot_grad - cum_grad) ** 2 / (tot_hess - cum_hess + l2_penalty)
                        - tot_grad * tot_grad / (tot_hess + l2_penalty)
                    )
                    gains_ref[q * 4 + m * 2 + e] = gain
                    best = jnp.maximum(best, gain)
            return best

        for m in range(2):
            pltpu.matmul_pop(acc[m])
        best = lax.fori_loop(
            0, owned // 4, quad, jnp.full((NODES, BINS), -jnp.inf, jnp.float32)
        )
        best = jnp.maximum(best[:, :LANES], best[:, LANES:])
        best = jnp.concatenate([best, jnp.zeros((LANES - NODES, LANES), jnp.float32)], axis=0)
        best_ref[...] = jnp.max(best.T, axis=0, keepdims=True)

    pl.run_scoped(
        lambda a, b: scan((a, b)),
        pltpu.ACC(0)((4 * 2 * NODES, BINS), jnp.float32),
        pltpu.ACC(1)((4 * 2 * NODES, BINS), jnp.float32),
    )


def body(mesh, bin_ids, gradients, hessians, node_ids, predictions, split_feature, split_bin):
    peers = mesh.shape["rows"]
    rows, feats = bin_ids.shape
    owned = feats // peers
    chunks = rows // LANES
    info = jnp.stack(
        [
            gradients.astype(jnp.float32),
            hessians.astype(jnp.float32),
            node_ids.astype(jnp.float32),
        ]
    ).reshape(3, chunks, LANES)
    split = jnp.stack([split_feature, split_bin], axis=1)
    depth = chunks * (owned + EXTRA)
    pay = pl.pallas_call(
        prep_kernel,
        out_shape=jax.ShapeDtypeStruct((peers, depth, LANES), jnp.float32),
        in_specs=[VMEM] * 4,
        out_specs=VMEM,
        name="prep",
    )(bin_ids, info, node_ids.reshape(chunks, LANES), split)
    got = lax.all_to_all(pay, "rows", 0, 0, tiled=True)
    mine = pay[0, chunks * owned :, :]
    gains, best, leaf_values, new_predictions = pl.pallas_call(
        hist_kernel,
        out_shape=(
            jax.ShapeDtypeStruct((owned, NODES, BINS), jnp.float32),
            jax.ShapeDtypeStruct((1, LANES), jnp.float32),
            jax.ShapeDtypeStruct((2, NODES), jnp.float32),
            jax.ShapeDtypeStruct((chunks, LANES), jnp.float32),
        ),
        in_specs=[VMEM] * 3,
        out_specs=(VMEM,) * 4,
        scratch_shapes=[pltpu.VMEM((peers, chunks, 2 * NODES, LANES), jnp.bfloat16)],
        name="hist",
    )(got, mine, predictions.reshape(chunks, LANES))
    spread = lax.all_to_all(
        jnp.broadcast_to(best, (peers, LANES)), "rows", 0, 0, tiled=True
    )
    best_gain = jnp.max(spread, axis=0)[:NODES]
    return gains, best_gain, leaf_values, new_predictions.reshape(rows)


def solution(mesh):
    rows = P(("groups", "rows"))
    return jax.shard_map(
        functools.partial(body, mesh),
        mesh=mesh,
        in_specs=(
            P(("groups", "rows"), None),
            rows,
            rows,
            rows,
            rows,
            P("groups"),
            P("groups"),
        ),
        out_specs=(
            P(("groups", "rows"), None, None),
            P("groups"),
            P(None, "groups"),
            rows,
        ),
        check_vma=False,
    )
```

time: 399 us -> 81.2 us (0.20)
  waiting for transfers between devices: 173 us -> 23.8 us
  matrix products: 87.4 us -> 0 us
  other arithmetic: 42 us -> 3.19 us
  blocking collectives: 48.7 us -> 13.7 us
  Pallas kernels: 0 us -> 28.4 us
  local copies, waits for them, and re-layouts: 21.3 us -> 3.65 us
  between operations: 14.9 us -> 0.64 us
  loops' own time: 11 us -> 0 us
  starting transfers between devices: 0.04 us -> 7.41 us
    reduce_scatter x1 -> x0, waiting for transfers between devices: 173 us -> none  [body(): lax.psum_scatter(full_terms, 'rows', scatter_dimension=0, tiled=True)]
    dot_general x16 -> x0, matrix products: 87.4 us -> none  [one_block(): jnp.einsum('rk,rfb->fkb', weights, bin_onehot(columns), preferred_element...]
    another operation x7 -> x4, other arithmetic: 37.4 us -> 2.66 us  [the longest x3 1.98 us: body(): jnp.stack([gradients.astype(jnp.float32), hessians.astype(jnp.float32), n...]
    unnamed x1 -> x0, blocking collectives: 31.5 us -> none
    pallas_call x0 -> x2, Pallas kernels: none -> 28.4 us  [the longest x1 25.8 us: body(): pl.pallas_call(hist_kernel, out_shape=(jax.ShapeDtypeStruct((owned, NODES...]
    all_to_all x0 -> x1, waiting for transfers between devices: none -> 23.8 us  [body(): got = lax.all_to_all(pay, 'rows', 0, 0, tiled=True)]
    all_gather x1 -> x0, blocking collectives: 17.2 us -> none  [combined_all(): gathered = jax.tree.map(lambda a: lax.all_gather(a, axis), part)]
    all_to_all x0 -> x1, blocking collectives: none -> 13.7 us  [body(): lax.all_to_all(jnp.broadcast_to(best, (peers, LANES)), 'rows', 0, 0, tile...]
  transfers between devices with their start and end apart: 1 -> 1, of which waited for: 1 -> 1; matrix products, arithmetic and copies ran while one was open for 1% -> 2% of each run, Pallas kernels for 0% -> 0%
where the time goes in v1:
time: 81.2 us; the launch traced here: 80.8 us
  Pallas kernels  28.4 us (35%)
  waiting for transfers between devices  23.8 us (29%)
  blocking collectives  13.7 us (17%)
  starting transfers between devices  7.41 us (9%)
  local copies, waits for them, and re-layouts  3.65 us (4%)
  other arithmetic  3.19 us (4%)
    pallas_call x1, Pallas kernels, body(): pl.pallas_call(hist_kernel, out_shape=(jax.ShapeDtypeStruct((owned, NODES...  25.8 us
    all_to_all x1, waiting for transfers between devices, body(): got = lax.all_to_all(pay, 'rows', 0, 0, tiled=True)  23.8 us
    all_to_all x1, blocking collectives, body(): lax.all_to_all(jnp.broadcast_to(best, (peers, LANES)), 'rows', 0, 0, tile...  13.7 us
    all_to_all x1, starting transfers between devices, body(): got = lax.all_to_all(pay, 'rows', 0, 0, tiled=True)  7.41 us
    pallas_call x1, Pallas kernels, body(): pl.pallas_call(prep_kernel, out_shape=jax.ShapeDtypeStruct((peers, depth,...  2.64 us
    another operation x3, other arithmetic, body(): jnp.stack([gradients.astype(jnp.float32), hessians.astype(jnp.float32), n...  1.98 us
  transfers between devices with their start and end apart: 1, of which 1 were waited for; matrix products, arithmetic and copies ran while one was open for 2% of the time, Pallas kernels for 0%

profile of v1, /device:TPU:0, one launch (start us, length us, event | category | flops | bytes accessed | tf_op | source)
XLA Modules:
  0.0 80.8 jit_solution(8877562872158556868)
XLA Ops:
  0.6 0.7 convert_bitcast_fusion
  1.3 0.7 pad_add_fusion
  2.0 0.7 copy.15.split_ref
  2.7 0.7 bitcast_convert_fusion
  3.4 0.6 pad_maximum_fusion.info_ref
  4.0 2.6 %prep.1 = f32[16,144,128]{2,1,0:T(8,128)} custom-call(s32[512,512]{1,0:T(8,128)} %bins_ref.1, f32[3,4,128]{2,1,0:T(4,128)} %pad_maximum_fusion.info_ref, s32[4,128]{1,0:T(4,128)} %bitcast.19, s32[16,2]{1,0:T(8,128)} %copy.15.split_ref), custom_call_target="tpu_custom_call" | custom-call | tf_op jit(solution)/shard_map/prep/pallas_call | solution.py:187
  6.6 7.4 %all-to-all-start = ((f32[16,144,128]{2,1,0:T(8,128)}), f32[16,144,128]{2,1,0:T(8,128)S(1)}, u32[]{:S(2)}, u32[]{:S(2)}) async-start(f32[16,144,128]{2,1,0:T(8,128)} %prep.1), calls=%async_computation | async-start | bytes 2359296 | tf_op jit(solution)/shard_map/all_to_all | solution.py:194
  14.0 1.3 %slice_bitcast_fusion.mine_ref = f32[16,128]{1,0:T(8,128)} fusion(f32[16,144,128]{2,1,0:T(8,128)} %prep.1), kind=kLoop, calls=%fused_computation | loop fusion | bytes 16384 | tf_op jit(solution)/shard_map/squeeze | solution.py:195
  15.3 23.8 %all-to-all-done.pay_ref = f32[16,144,128]{2,1,0:T(8,128)S(1)} async-done(((f32[16,144,128]{2,1,0:T(8,128)}), f32[16,144,128]{2,1,0:T(8,128)S(1)}, u32[]{:S(2)}, u32[]{:S(2)}) %all-to-all-start) | async-done | bytes 1179680 | tf_op jit(solution)/shard_map/all_to_all | solution.py:194
  39.1 0.0 copy-start
  39.1 1.0 %copy-done = f32[16,144,128]{2,1,0:T(8,128)} copy-done((f32[16,144,128]{2,1,0:T(8,128)}, f32[16,144,128]{2,1,0:T(8,128)S(1)}, u32[]{:S(2)}) %copy-start) | copy-done | bytes 1179672
  40.1 25.8 %hist.1 = (f32[32,16,256]{2,1,0:T(8,128)}, f32[1,128]{1,0:T(1,128)}, f32[2,16]{1,0:T(2,128)}, f32[4,128]{1,0:T(4,128)}) custom-call(f32[16,144,128]{2,1,0:T(8,128)} %copy-done, f32[16,128]{1,0:T(8,128)} %slice_bitcast_fusion.mine_ref, f32[4,128]{1,0:T(4,128)} %bitcast.20), custom_call_target="tpu_custom_call" | custom-call | tf_op jit(solution)/shard_map/hist/pallas_call | solution.py:196
  65.9 0.7 broadcast_in_dim.2
  66.6 13.7 %all_to_all.11 = f32[16,1,128]{2,1,0:T(1,128)S(1)} all-to-all(f32[16,1,128]{2,1,0:T(1,128)S(1)} %broadcast_in_dim.2), channel_id=1, replica_groups=mesh['groups'=2,'rows'=16] {'rows'}, dimensions={0} | all-to-all | bytes 16384 | tf_op jit(solution)/shard_map/all_to_all | solution.py:209
  80.2 0.5 reduce_max.9
Async XLA Ops:
  6.6 32.5 %all-to-all-start = ((f32[16,144,128]{2,1,0:T(8,128)}), f32[16,144,128]{2,1,0:T(8,128)S(1)}, u32[]{:S(2)}, u32[]{:S(2)}) async-start(f32[16,144,128]{2,1,0:T(8,128)} %prep.1), calls=%async_computation | async-start | bytes 2359296 | tf_op jit(solution)/shard_map/all_to_all | solution.py:194
  39.1 1.0 %copy-start = (f32[16,144,128]{2,1,0:T(8,128)}, f32[16,144,128]{2,1,0:T(8,128)S(1)}, u32[]{:S(2)}) copy-start(f32[16,144,128]{2,1,0:T(8,128)S(1)} %all-to-all-done.pay_ref) | copy-start | bytes 3538948

commit v2 on v1

v2 whole, which is shorter than its diff:
```python
import functools

import jax
import jax.numpy as jnp
from jax import lax
from jax.experimental import pallas as pl
from jax.experimental.pallas import tpu as pltpu
from jax.sharding import PartitionSpec as P

BINS = 256
NODES = 16
LANES = 128
HALF = BINS // 2
EXTRA = 4
QUAD = 4
BLOCK = 16

l2_penalty = 1.0
shrinkage = 0.5

VMEM = pl.BlockSpec(memory_space=pltpu.VMEM)
SMEM = pl.BlockSpec(memory_space=pltpu.SMEM)
PARAMS = pltpu.CompilerParams(vmem_limit_bytes=16 * 1024 * 1024)


def prep_kernel(bins_ref, grad_ref, hess_ref, node_ref, feat_ref, cut_ref, pay_ref, own_ref):
    peers = pay_ref.shape[0]
    rows, feats = bins_ref.shape
    owned = feats // peers
    chunks = rows // LANES
    base = chunks * owned
    node_col = lax.broadcasted_iota(jnp.int32, (NODES, LANES), 0)
    feat_pos = lax.broadcasted_iota(jnp.int32, (NODES, feats), 1)
    node_pos = lax.broadcasted_iota(jnp.int32, (NODES, feats), 0)
    wanted = jnp.zeros((NODES, feats), jnp.int32)
    cut = jnp.zeros((NODES, LANES), jnp.int32)
    for n in range(NODES):
        wanted = jnp.where(node_pos == n, feat_ref[n], wanted)
        cut = jnp.where(node_col == n, cut_ref[n], cut)
    cut = cut.astype(jnp.float32)
    pick = jnp.where(feat_pos == wanted, 1.0, 0.0).astype(jnp.bfloat16)
    for c in range(chunks):
        span = slice(c * LANES, (c + 1) * LANES)
        block = bins_ref[span, :].astype(jnp.float32)
        picked = lax.dot_general(
            pick,
            block.astype(jnp.bfloat16),
            (((1,), (1,)), ((), ())),
            preferred_element_type=jnp.float32,
        )
        node = node_ref[span].reshape(1, LANES)
        member = node == node_col
        side = jnp.sum(
            jnp.where(member & (picked > cut), 1.0, 0.0), axis=0, keepdims=True
        )
        info = [
            grad_ref[span].astype(jnp.float32).reshape(1, LANES),
            hess_ref[span].astype(jnp.float32).reshape(1, LANES),
            node.astype(jnp.float32),
            side,
        ]
        for k in range(EXTRA):
            own_ref[k * chunks + c : k * chunks + c + 1, :] = info[k]
        flipped = block.T
        for d in range(peers):
            pay_ref[d, c * owned : (c + 1) * owned, :] = flipped[d * owned : (d + 1) * owned, :]
    info = own_ref[...]
    for d in range(peers):
        pay_ref[d, base:, :] = info


def weigh(pay_ref, base, chunks, w_ref):
    f32 = jnp.float32
    node_col = lax.broadcasted_iota(jnp.int32, (NODES, LANES), 0).astype(f32)

    def build(s, sums):
        out = list(sums)
        for c in range(chunks):
            g, h, node, side = (
                pay_ref[s, base + k * chunks + c : base + k * chunks + c + 1, :]
                for k in range(EXTRA)
            )
            member = node == node_col
            wg = jnp.where(member, g, 0.0)
            wh = jnp.where(member, h, 0.0)
            w_ref[s, c] = jnp.concatenate([wg, wh], axis=0).astype(jnp.bfloat16)
            left = side < 0.5
            out[0] = out[0] + jnp.where(left, wg, 0.0)
            out[1] = out[1] + jnp.where(left, wh, 0.0)
            out[2] = out[2] + wg
            out[3] = out[3] + wh
        return tuple(out)

    zero = jnp.zeros((NODES, LANES), f32)
    return lax.fori_loop(0, pay_ref.shape[0], build, (zero,) * 4)


def settle(sums, chunks, own_ref, pred_ref, leaf_ref, new_ref):
    left_grad, left_hess, node_grad, node_hess = (
        jnp.sum(x, axis=1, keepdims=True) for x in sums
    )
    node_col = lax.broadcasted_iota(jnp.int32, (NODES, LANES), 0).astype(jnp.float32)
    leaf_left = -left_grad / (left_hess + l2_penalty)
    leaf_right = -(node_grad - left_grad) / (node_hess - left_hess + l2_penalty)
    lane = lax.broadcasted_iota(jnp.int32, (NODES, LANES), 1)
    both = jnp.where(lane == 0, leaf_left, leaf_right)
    both = jnp.concatenate([both, jnp.zeros((LANES - NODES, LANES), jnp.float32)], axis=0)
    leaf_ref[...] = both.T[0:2, 0:NODES]
    for c in range(chunks):
        span = slice(c * LANES, (c + 1) * LANES)
        node = own_ref[2 * chunks + c : 2 * chunks + c + 1, :]
        side = own_ref[3 * chunks + c : 3 * chunks + c + 1, :]
        value = jnp.where(side < 0.5, leaf_left, leaf_right)
        value = jnp.sum(jnp.where(node == node_col, value, 0.0), axis=0, keepdims=True)
        new_ref[span] = pred_ref[span] + shrinkage * value.reshape(LANES)


def sweep(pay_ref, w_ref, owned, chunks, finish, carry):
    f8, i16 = jnp.float8_e4m3fn, jnp.int16
    peers = pay_ref.shape[0]
    block = min(peers, BLOCK)
    quads = owned // QUAD
    group = min(4, quads)
    spot = lax.broadcasted_iota(jnp.int32, (32, LANES), 0)
    steps = [(spot + 32 * i).astype(i16) for i in range(HALF // 32)]
    one = jnp.ones((32, LANES), f8)
    nil = jnp.zeros((32, LANES), f8)
    none = jnp.zeros((NODES, LANES), jnp.bfloat16)

    def terms(s, c, f):
        row = pay_ref[s, pl.ds(c * owned + f, 1), :].astype(jnp.int32)
        bins = jnp.broadcast_to(row, (NODES, LANES)).astype(i16)
        high16 = bins >= i16(HALF)
        low = jnp.where(high16, bins - i16(HALF), bins)
        low = jnp.concatenate([low, low], axis=0)
        rhs = jnp.concatenate([jnp.where(low <= t, one, nil) for t in steps], axis=0)
        wg, wh = w_ref[s, c, 0:NODES, :], w_ref[s, c, NODES : 2 * NODES, :]
        upper = high16
        lhs = jnp.concatenate(
            [
                jnp.where(upper, none, wg),
                jnp.where(upper, none, wh),
                jnp.where(upper, wg, none),
                jnp.where(upper, wh, none),
            ],
            axis=0,
        )
        return lhs, rhs

    def tile(s, t, f):
        part = [[terms(s, 2 * t + i, f + e) for i in range(2)] for e in range(2)]
        return [
            jnp.concatenate(
                [jnp.concatenate([p[k] for p in e], axis=1) for e in part], axis=0
            )
            for k in range(2)
        ]

    def sources(at, q, acc):
        for s in range(block):
            for t in range(chunks // 2):
                reg = (s * (chunks // 2) + t) % 2
                for m in range(2):
                    lhs, rhs = tile(at + s, t, q * QUAD + m * 2)
                    pltpu.matmul_push_rhs(rhs, staging_register=reg, mxu_index=m, transpose=True)
                    pltpu.matmul_acc_lhs(acc[m], lhs, load_staged_rhs=reg)

    def matmuls(q, acc):
        if peers == block:
            sources(0, q, acc)
        else:
            lax.fori_loop(
                0, peers // block, lambda b, x: (sources(b * block, q, acc), x)[1], 0
            )

    def scan(*acc):
        sets = (acc[0:2], acc[2:4])

        def step(j, carry):
            for i in range(group):
                matmuls(j * group + i, sets[i % 2])
                if i:
                    carry = finish(j * group + i - 1, sets[(i - 1) % 2], carry)
            return finish(j * group + group - 1, sets[(group - 1) % 2], carry)

        for a in acc:
            pltpu.matmul_pop(a)
        return lax.fori_loop(0, quads // group, step, carry)

    shape = ((4 * 2 * NODES, BINS), jnp.float32)
    return pl.run_scoped(
        scan, pltpu.ACC(0)(*shape), pltpu.ACC(1)(*shape), pltpu.ACC(0)(*shape), pltpu.ACC(1)(*shape)
    )


def hist_kernel(chunks, pay_ref, own_ref, pred_ref, gains_ref, best_ref, leaf_ref, new_ref, w_ref):
    peers = pay_ref.shape[0]
    owned = gains_ref.shape[0]
    base = chunks * owned
    sums = weigh(pay_ref, base, chunks, w_ref)
    settle(sums, chunks, own_ref, pred_ref, leaf_ref, new_ref)
    def finish(q, acc, best):
        for m in range(2):
            out = pltpu.matmul_pop(acc[m])
            for e in range(2):
                c = out[e * 64 : (e + 1) * 64, e * HALF : (e + 1) * HALF]
                cum_grad, cum_hess = (
                    jnp.concatenate([a, b + a[:, HALF - 1 : HALF]], axis=1)
                    for a, b in ((c[0:16], c[32:48]), (c[16:32], c[48:64]))
                )
                tot_grad = cum_grad[:, BINS - 1 : BINS]
                tot_hess = cum_hess[:, BINS - 1 : BINS]
                gain = 0.5 * (
                    cum_grad * cum_grad / (cum_hess + l2_penalty)
                    + (tot_grad - cum_grad) ** 2 / (tot_hess - cum_hess + l2_penalty)
                    - tot_grad * tot_grad / (tot_hess + l2_penalty)
                )
                gains_ref[q * QUAD + m * 2 + e] = gain
                best = jnp.maximum(best, gain)
        return best

    best = sweep(
        pay_ref, w_ref, owned, chunks, finish, jnp.full((NODES, BINS), -jnp.inf, jnp.float32)
    )
    best = jnp.maximum(best[:, :LANES], best[:, LANES:])
    best = jnp.concatenate([best, jnp.zeros((LANES - NODES, LANES), jnp.float32)], axis=0)
    row = jnp.max(best.T, axis=0, keepdims=True)
    for d in range(peers):
        best_ref[d] = row


def body(mesh, bin_ids, gradients, hessians, node_ids, predictions, split_feature, split_bin):
    peers = mesh.shape["rows"]
    rows, feats = bin_ids.shape
    owned = feats // peers
    chunks = rows // LANES
    f32 = jnp.float32
    depth = chunks * (owned + EXTRA)
    pay, own = pl.pallas_call(
        prep_kernel,
        out_shape=[
            jax.ShapeDtypeStruct((peers, depth, LANES), f32),
            jax.ShapeDtypeStruct((chunks * EXTRA, LANES), f32),
        ],
        in_specs=[VMEM] * 4 + [SMEM] * 2,
        out_specs=[VMEM] * 2,
        name="prep",
    )(bin_ids, gradients, hessians, node_ids, split_feature, split_bin)
    got = lax.all_to_all(pay, "rows", 0, 0, tiled=True)
    gains, best, leaf_values, new_predictions = pl.pallas_call(
        functools.partial(hist_kernel, chunks),
        out_shape=(
            jax.ShapeDtypeStruct((owned, NODES, BINS), f32),
            jax.ShapeDtypeStruct((peers, 1, LANES), f32),
            jax.ShapeDtypeStruct((2, NODES), f32),
            jax.ShapeDtypeStruct((rows,), f32),
        ),
        in_specs=[VMEM] * 3,
        out_specs=(VMEM,) * 4,
        scratch_shapes=[pltpu.VMEM((peers, chunks, 2 * NODES, LANES), jnp.bfloat16)],
        compiler_params=PARAMS,
        name="hist",
    )(got, own, predictions)
    spread = lax.all_to_all(best, "rows", 0, 0, tiled=True)
    best_gain = jnp.max(spread, axis=(0, 1))[:NODES]
    return gains, best_gain, leaf_values, new_predictions


def solution(mesh):
    rows = P(("groups", "rows"))
    return jax.shard_map(
        functools.partial(body, mesh),
        mesh=mesh,
        in_specs=(
            P(("groups", "rows"), None),
            rows,
            rows,
            rows,
            rows,
            P("groups"),
            P("groups"),
        ),
        out_specs=(
            P(("groups", "rows"), None, None),
            P("groups"),
            P(None, "groups"),
            rows,
        ),
        check_vma=False,
    )
```

time: 81.2 us -> 61.2 us (0.75)
  blocking collectives: 13.7 us -> 46.5 us
  waiting for transfers between devices: 23.8 us -> 0 us
  Pallas kernels: 28.4 us -> 13.3 us
  starting transfers between devices: 7.41 us -> 0 us
  local copies, waits for them, and re-layouts: 3.65 us -> 0.01 us
  other arithmetic: 3.19 us -> 0.54 us
    all_to_all x1 -> x2, blocking collectives: 13.7 us -> 46.5 us  [the longest x1 37.1 us: body(): got = lax.all_to_all(pay, 'rows', 0, 0, tiled=True)]
    all_to_all x1 -> x0, waiting for transfers between devices: 23.8 us -> none  [body(): got = lax.all_to_all(pay, 'rows', 0, 0, tiled=True)]
    pallas_call x2, Pallas kernels: 28.4 us -> 13.3 us  [the longest x1 10.6 us: body(): pl.pallas_call(functools.partial(hist_kernel, chunks), out_shape=(jax.Sha...]
    all_to_all x1 -> x0, starting transfers between devices: 7.41 us -> none  [body(): got = lax.all_to_all(pay, 'rows', 0, 0, tiled=True)]
    another operation x4 -> x0, other arithmetic: 2.66 us -> none  [the longest x3 1.98 us: body(): jnp.stack([gradients.astype(jnp.float32), hessians.astype(jnp.float32), n...]
    squeeze x1 -> x0, local copies, waits for them, and re-layouts: 1.29 us -> none  [body(): mine = pay[0, chunks * owned:, :]]
    unnamed x2 -> x4, local copies, waits for them, and re-layouts: 1.02 us -> 0.01 us
  transfers between devices with their start and end apart: 1 -> 0, of which waited for: 1 -> 0; matrix products, arithmetic and copies ran while one was open for 2% -> 0% of each run, Pallas kernels for 0% -> 0%
where the time goes in v2:
time: 61.2 us; the launch traced here: 61 us
  blocking collectives  46.5 us (76%)
  Pallas kernels  13.3 us (22%)
  between operations  0.64 us (1%)
    all_to_all x1, blocking collectives, body(): got = lax.all_to_all(pay, 'rows', 0, 0, tiled=True)  37.1 us
    pallas_call x1, Pallas kernels, body(): pl.pallas_call(functools.partial(hist_kernel, chunks), out_shape=(jax.Sha...  10.6 us
    all_to_all x1, blocking collectives, body(): spread = lax.all_to_all(best, 'rows', 0, 0, tiled=True)  9.44 us
    pallas_call x1, Pallas kernels, body(): pl.pallas_call(prep_kernel, out_shape=[jax.ShapeDtypeStruct((peers, depth...  2.61 us

profile of v2, /device:TPU:0, one launch (start us, length us, event | category | flops | bytes accessed | tf_op | source)
XLA Modules:
  0.0 61.0 jit_solution(9533849333193914317)
XLA Ops:
  0.6 2.6 %prep.1 = (f32[16,144,128]{2,1,0:T(8,128)}, f32[16,128]{1,0:T(8,128)}) custom-call(s32[512,512]{1,0:T(8,128)} %bins_ref.1, bf16[512]{0:T(512)(128)(2,1)} %grad_ref.1, bf16[512]{0:T(512)(128)(2,1)} %hess_ref.1, s32[512]{0:T(512)} %node_ref.1, s32[16]{0:T(128)} %feat_ref.1, s32[16]{0:T(128)} %cut_ref.1), custom_call_target="tpu_custom_call" | custom-call | tf_op jit(solution)/shard_map/prep/pallas_call | solution.py:239
  3.2 0.0 copy-start
  3.2 0.0 copy-start.1
  3.3 37.1 %all_to_all.10.pay_ref = f32[16,144,128]{2,1,0:T(8,128)S(1)} all-to-all(f32[16,144,128]{2,1,0:T(8,128)} %get-tuple-element.10), channel_id=1, replica_groups=mesh['groups'=2,'rows'=16] {'rows'}, dimensions={0} | all-to-all | bytes 2359296 | tf_op jit(solution)/shard_map/all_to_all | solution.py:249
  40.3 0.0 copy-done
  40.3 0.0 copy-done.1
  40.3 10.6 %hist.1 = (f32[32,16,256]{2,1,0:T(8,128)}, f32[16,1,128]{2,1,0:T(1,128)S(1)}, f32[2,16]{1,0:T(2,128)}, f32[512]{0:T(512)}) custom-call(f32[16,144,128]{2,1,0:T(8,128)S(1)} %all_to_all.10.pay_ref, f32[16,128]{1,0:T(8,128)S(1)} %copy-done, f32[512]{0:T(512)S(1)} %copy-done.1), custom_call_target="tpu_custom_call" | custom-call | tf_op jit(solution)/shard_map/hist/pallas_call | solution.py:250
  51.0 9.4 %all_to_all.11 = f32[16,1,128]{2,1,0:T(1,128)S(1)} all-to-all(f32[16,1,128]{2,1,0:T(1,128)S(1)} %get-tuple-element.13), channel_id=1, replica_groups=mesh['groups'=2,'rows'=16] {'rows'}, dimensions={0} | all-to-all | bytes 16384 | tf_op jit(solution)/shard_map/all_to_all | solution.py:264
  60.4 0.5 reduce_max.9
Async XLA Ops:
  3.2 37.1 %copy-start = (f32[16,128]{1,0:T(8,128)S(1)}, f32[16,128]{1,0:T(8,128)}, u32[]{:S(2)}) copy-start(f32[16,128]{1,0:T(8,128)} %get-tuple-element.11.own_ref) | copy-start | bytes 24580
  3.2 37.1 %copy-start.1 = (f32[512]{0:T(512)S(1)}, f32[512]{0:T(512)}, u32[]{:S(2)}) copy-start(f32[512]{0:T(512)} %pred_ref.1) | copy-start | bytes 6148

commit v3 on v2

--- a/solution.py
+++ b/solution.py
@@ -14,21 +14,58 @@
 EXTRA = 4
 QUAD = 4
 BLOCK = 16
+MOST_HOPS = 16
+
 
 l2_penalty = 1.0
 shrinkage = 0.5
 
 VMEM = pl.BlockSpec(memory_space=pltpu.VMEM)
-SMEM = pl.BlockSpec(memory_space=pltpu.SMEM)
+HBM = pl.BlockSpec(memory_space=pltpu.HBM)
 PARAMS = pltpu.CompilerParams(vmem_limit_bytes=16 * 1024 * 1024)
 
 
-def prep_kernel(bins_ref, grad_ref, hess_ref, node_ref, feat_ref, cut_ref, pay_ref, own_ref):
-    peers = pay_ref.shape[0]
+def hop_order(peers):
+    far = list(range(peers - 1, peers // 2 - 1, -1))
+    near = list(range(peers // 2 - 1, 0, -1))
+    split = max(len(near) - 3, 0)
+    return far[:4] + near[split:] + far[4:] + near[:split]
+
+
+def stage_hops(peers):
+    order = [0] + hop_order(peers)
+    half, quarter = peers // 2, peers // 4
+    return [order[:half], order[half : half + quarter], order[half + quarter :]]
+
+
+def prep_kernel(peers, bins_hbm, *refs):
+    inputs, outs, scratch = refs[:6], refs[6:-10], refs[-10:]
+    own_ref, block_refs = outs[0], outs[1:]
+    bins_ref, grad_ref, hess_ref, node_ref, pred_ref, feat_ref, cut_ref = scratch[:7]
+    pay_ref, bin_sems, sems = scratch[7:]
     rows, feats = bins_ref.shape
     owned = feats // peers
     chunks = rows // LANES
     base = chunks * owned
+    small = [
+        pltpu.make_async_copy(src, dst, sems.at[i])
+        for i, (src, dst) in enumerate(
+            zip(inputs, (grad_ref, hess_ref, node_ref, pred_ref, feat_ref, cut_ref))
+        )
+    ]
+    large = [
+        pltpu.make_async_copy(
+            bins_hbm.at[pl.ds(c * LANES, LANES), :],
+            bins_ref.at[pl.ds(c * LANES, LANES), :],
+            bin_sems.at[c],
+        )
+        for c in range(chunks)
+    ]
+    for copy in small + large:
+        copy.start()
+    for copy in small:
+        copy.wait()
+    target = block_refs[0] if peers > MOST_HOPS else pay_ref
     node_col = lax.broadcasted_iota(jnp.int32, (NODES, LANES), 0)
     feat_pos = lax.broadcasted_iota(jnp.int32, (NODES, feats), 1)
     node_pos = lax.broadcasted_iota(jnp.int32, (NODES, feats), 0)
@@ -40,6 +77,7 @@
     cut = cut.astype(jnp.float32)
     pick = jnp.where(feat_pos == wanted, 1.0, 0.0).astype(jnp.bfloat16)
     for c in range(chunks):
+        large[c].wait()
         span = slice(c * LANES, (c + 1) * LANES)
         block = bins_ref[span, :].astype(jnp.float32)
         picked = lax.dot_general(
@@ -58,44 +96,56 @@
             hess_ref[span].astype(jnp.float32).reshape(1, LANES),
             node.astype(jnp.float32),
             side,
+            pred_ref[span].reshape(1, LANES),
         ]
-        for k in range(EXTRA):
+        for k in range(EXTRA + 1):
             own_ref[k * chunks + c : k * chunks + c + 1, :] = info[k]
         flipped = block.T
         for d in range(peers):
-            pay_ref[d, c * owned : (c + 1) * owned, :] = flipped[d * owned : (d + 1) * owned, :]
-    info = own_ref[...]
-    for d in range(peers):
-        pay_ref[d, base:, :] = info
-
-
-def weigh(pay_ref, base, chunks, w_ref):
-    f32 = jnp.float32
-    node_col = lax.broadcasted_iota(jnp.int32, (NODES, LANES), 0).astype(f32)
-
-    def build(s, sums):
-        out = list(sums)
-        for c in range(chunks):
-            g, h, node, side = (
-                pay_ref[s, base + k * chunks + c : base + k * chunks + c + 1, :]
-                for k in range(EXTRA)
-            )
-            member = node == node_col
-            wg = jnp.where(member, g, 0.0)
-            wh = jnp.where(member, h, 0.0)
-            w_ref[s, c] = jnp.concatenate([wg, wh], axis=0).astype(jnp.bfloat16)
-            left = side < 0.5
-            out[0] = out[0] + jnp.where(left, wg, 0.0)
-            out[1] = out[1] + jnp.where(left, wh, 0.0)
-            out[2] = out[2] + wg
-            out[3] = out[3] + wh
-        return tuple(out)
-
-    zero = jnp.zeros((NODES, LANES), f32)
-    return lax.fori_loop(0, pay_ref.shape[0], build, (zero,) * 4)
-
-
-def settle(sums, chunks, own_ref, pred_ref, leaf_ref, new_ref):
+            target[d, c * owned : (c + 1) * owned, :] = flipped[d * owned : (d + 1) * owned, :]
+    info = own_ref[0 : EXTRA * chunks, :]
+    if peers > MOST_HOPS:
+        for d in range(peers):
+            target[d, base:, :] = info
+    else:
+        me = lax.axis_index("rows")
+        for k, block_ref in enumerate(block_refs):
+            block_ref[0:base, :] = target[me ^ k, 0:base, :]
+            block_ref[base:, :] = info
+
+
+def weigh(read, s, base, chunks, w_ref, sums):
+    node_col = lax.broadcasted_iota(jnp.int32, (NODES, LANES), 0).astype(jnp.float32)
+    out = list(sums)
+    for c in range(chunks):
+        g, h, node, side = (read(s, base + k * chunks + c) for k in range(EXTRA))
+        member = node == node_col
+        wg = jnp.where(member, g, 0.0)
+        wh = jnp.where(member, h, 0.0)
+        w_ref[s, c] = jnp.concatenate([wg, wh], axis=0).astype(jnp.bfloat16)
+        left = side < 0.5
+        out[0] = out[0] + jnp.where(left, wg, 0.0)
+        out[1] = out[1] + jnp.where(left, wh, 0.0)
+        out[2] = out[2] + wg
+        out[3] = out[3] + wh
+    return tuple(out)
+
+
+def weigh_all(read, count, base, chunks, w_ref, sums):
+    if count <= MOST_HOPS:
+        for s in range(count):
+            sums = weigh(read, s, base, chunks, w_ref, sums)
+        return sums
+    return lax.fori_loop(
+        0, count, lambda s, x: weigh(read, s, base, chunks, w_ref, x), tuple(sums)
+    )
+
+
+def no_sums():
+    return (jnp.zeros((NODES, LANES), jnp.float32),) * 4
+
+
+def settle(sums, chunks, own_ref, leaf_ref, new_ref):
     left_grad, left_hess, node_grad, node_hess = (
         jnp.sum(x, axis=1, keepdims=True) for x in sums
     )
@@ -112,13 +162,13 @@
         side = own_ref[3 * chunks + c : 3 * chunks + c + 1, :]
         value = jnp.where(side < 0.5, leaf_left, leaf_right)
         value = jnp.sum(jnp.where(node == node_col, value, 0.0), axis=0, keepdims=True)
-        new_ref[span] = pred_ref[span] + shrinkage * value.reshape(LANES)
-
-
-def sweep(pay_ref, w_ref, owned, chunks, finish, carry):
+        pred = own_ref[EXTRA * chunks + c : EXTRA * chunks + c + 1, :]
+        new_ref[span] = (pred + shrinkage * value).reshape(LANES)
+
+
+def sweep(read, count, w_ref, owned, chunks, finish, carry):
     f8, i16 = jnp.float8_e4m3fn, jnp.int16
-    peers = pay_ref.shape[0]
-    block = min(peers, BLOCK)
+    block = min(count, BLOCK)
     quads = owned // QUAD
     group = min(4, quads)
     spot = lax.broadcasted_iota(jnp.int32, (32, LANES), 0)
@@ -128,7 +178,7 @@
     none = jnp.zeros((NODES, LANES), jnp.bfloat16)
 
     def terms(s, c, f):
-        row = pay_ref[s, pl.ds(c * owned + f, 1), :].astype(jnp.int32)
+        row = read(s, c * owned + f).astype(jnp.int32)
         bins = jnp.broadcast_to(row, (NODES, LANES)).astype(i16)
         high16 = bins >= i16(HALF)
         low = jnp.where(high16, bins - i16(HALF), bins)
@@ -166,11 +216,11 @@
                     pltpu.matmul_acc_lhs(acc[m], lhs, load_staged_rhs=reg)
 
     def matmuls(q, acc):
-        if peers == block:
+        if count == block:
             sources(0, q, acc)
         else:
             lax.fori_loop(
-                0, peers // block, lambda b, x: (sources(b * block, q, acc), x)[1], 0
+                0, count // block, lambda b, x: (sources(b * block, q, acc), x)[1], 0
             )
 
     def scan(*acc):
@@ -193,17 +243,56 @@
     )
 
 
-def hist_kernel(chunks, pay_ref, own_ref, pred_ref, gains_ref, best_ref, leaf_ref, new_ref, w_ref):
-    peers = pay_ref.shape[0]
+def reader(refs):
+    if len(refs) == 1:
+        return lambda s, r: refs[0][s, pl.ds(r, 1), :]
+    return lambda s, r: refs[s][pl.ds(r, 1), :]
+
+
+def stage_kernel(chunks, sources, *refs):
+    block_refs, before, (part_ref, sums_ref, w_ref) = refs[:sources], refs[sources:-3], refs[-3:]
+    owned = part_ref.shape[0]
+    read = reader(block_refs)
+    sums = tuple(before[1][k] for k in range(4)) if before else no_sums()
+    sums = weigh_all(read, sources, chunks * owned, chunks, w_ref, sums)
+    for k in range(4):
+        sums_ref[k] = sums[k]
+
+    def finish(q, acc, carry):
+        for m in range(2):
+            out = pltpu.matmul_pop(acc[m])
+            for e in range(2):
+                f = q * QUAD + m * 2 + e
+                c = out[e * 64 : (e + 1) * 64, e * HALF : (e + 1) * HALF]
+                part_ref[f] = c + before[0][f] if before else c
+        return carry
+
+    sweep(read, sources, w_ref, owned, chunks, finish, 0)
+
+
+def last_kernel(chunks, split, *refs):
+    gains_ref, best_ref, leaf_ref, new_ref, w_ref = refs[-5:]
+    own_ref = refs[-6]
+    block_refs = refs[:-6]
+    sums = no_sums()
+    if split:
+        part_ref, sums_ref = refs[-8:-6]
+        block_refs = refs[:-8]
+        sums = tuple(sums_ref[k] for k in range(4))
+    peers = best_ref.shape[0]
     owned = gains_ref.shape[0]
-    base = chunks * owned
-    sums = weigh(pay_ref, base, chunks, w_ref)
-    settle(sums, chunks, own_ref, pred_ref, leaf_ref, new_ref)
+    read = reader(block_refs)
+    count = len(block_refs) if len(block_refs) > 1 else peers
+    sums = weigh_all(read, count, chunks * owned, chunks, w_ref, sums)
+    settle(sums, chunks, own_ref, leaf_ref, new_ref)
+
     def finish(q, acc, best):
         for m in range(2):
             out = pltpu.matmul_pop(acc[m])
             for e in range(2):
                 c = out[e * 64 : (e + 1) * 64, e * HALF : (e + 1) * HALF]
+                if split:
+                    c = c + part_ref[q * QUAD + m * 2 + e]
                 cum_grad, cum_hess = (
                     jnp.concatenate([a, b + a[:, HALF - 1 : HALF]], axis=1)
                     for a, b in ((c[0:16], c[32:48]), (c[16:32], c[48:64]))
@@ -219,9 +308,8 @@
                 best = jnp.maximum(best, gain)
         return best
 
-    best = sweep(
-        pay_ref, w_ref, owned, chunks, finish, jnp.full((NODES, BINS), -jnp.inf, jnp.float32)
-    )
+    least = jnp.full((NODES, BINS), -jnp.inf, jnp.float32)
+    best = sweep(read, count, w_ref, owned, chunks, finish, least)
     best = jnp.maximum(best[:, :LANES], best[:, LANES:])
     best = jnp.concatenate([best, jnp.zeros((LANES - NODES, LANES), jnp.float32)], axis=0)
     row = jnp.max(best.T, axis=0, keepdims=True)
@@ -236,31 +324,78 @@
     chunks = rows // LANES
     f32 = jnp.float32
     depth = chunks * (owned + EXTRA)
-    pay, own = pl.pallas_call(
-        prep_kernel,
-        out_shape=[
-            jax.ShapeDtypeStruct((peers, depth, LANES), f32),
-            jax.ShapeDtypeStruct((chunks * EXTRA, LANES), f32),
+    hops = hop_order(peers) if peers <= MOST_HOPS else []
+    many = jax.ShapeDtypeStruct((peers, depth, LANES), f32)
+    single = jax.ShapeDtypeStruct((depth, LANES), f32)
+
+    def cost(sources):
+        work = 2 * sources * rows * owned * 2 * NODES * BINS
+        return pl.CostEstimate(flops=work, bytes_accessed=work // 4096, transcendentals=0)
+
+    def weights(sources):
+        return pltpu.VMEM((sources, chunks, 2 * NODES, LANES), jnp.bfloat16)
+
+    own, *blocks = pl.pallas_call(
+        functools.partial(prep_kernel, peers),
+        out_shape=[jax.ShapeDtypeStruct((chunks * (EXTRA + 1), LANES), f32)]
+        + ([single] * peers if hops else [many]),
+        in_specs=[HBM] * 7,
+        out_specs=[VMEM] * (1 + (peers if hops else 1)),
+        scratch_shapes=[
+            pltpu.VMEM((rows, feats), jnp.int32),
+            pltpu.VMEM((rows,), gradients.dtype),
+            pltpu.VMEM((rows,), hessians.dtype),
+            pltpu.VMEM((rows,), jnp.int32),
+            pltpu.VMEM((rows,), f32),
+            pltpu.SMEM((NODES,), jnp.int32),
+            pltpu.SMEM((NODES,), jnp.int32),
+            pltpu.VMEM((peers if hops else 1, depth, LANES), f32),
+            pltpu.SemaphoreType.DMA((chunks,)),
+            pltpu.SemaphoreType.DMA((6,)),
         ],
-        in_specs=[VMEM] * 4 + [SMEM] * 2,
-        out_specs=[VMEM] * 2,
         name="prep",
-    )(bin_ids, gradients, hessians, node_ids, split_feature, split_bin)
-    got = lax.all_to_all(pay, "rows", 0, 0, tiled=True)
+    )(bin_ids, gradients, hessians, node_ids, predictions, split_feature, split_bin)
+    if hops:
+        landed = {0: blocks[0]}
+        for k in hops:
+            landed[k] = lax.ppermute(
+                blocks[k], "rows", [(i, i ^ k) for i in range(peers)]
+            )
+        part = []
+        stages = stage_hops(peers)
+        for group in stages[:-1]:
+            part = pl.pallas_call(
+                functools.partial(stage_kernel, chunks, len(group)),
+                out_shape=(
+                    jax.ShapeDtypeStruct((owned, 4 * NODES, HALF), f32),
+                    jax.ShapeDtypeStruct((4, NODES, LANES), f32),
+                ),
+                in_specs=[VMEM] * (len(group) + len(part)),
+                out_specs=(VMEM, VMEM),
+                scratch_shapes=[weights(len(group))],
+                compiler_params=PARAMS,
+                cost_estimate=cost(len(group)),
+            )(*[landed[k] for k in group], *part)
+        late = stages[-1]
+        operands = [landed[k] for k in late] + list(part)
+    else:
+        operands = [lax.all_to_all(blocks[0], "rows", 0, 0, tiled=True)]
+    count = len(late) if hops else peers
     gains, best, leaf_values, new_predictions = pl.pallas_call(
-        functools.partial(hist_kernel, chunks),
+        functools.partial(last_kernel, chunks, bool(hops)),
         out_shape=(
             jax.ShapeDtypeStruct((owned, NODES, BINS), f32),
             jax.ShapeDtypeStruct((peers, 1, LANES), f32),
             jax.ShapeDtypeStruct((2, NODES), f32),
             jax.ShapeDtypeStruct((rows,), f32),
         ),
-        in_specs=[VMEM] * 3,
+        in_specs=[VMEM] * (len(operands) + 1),
         out_specs=(VMEM,) * 4,
-        scratch_shapes=[pltpu.VMEM((peers, chunks, 2 * NODES, LANES), jnp.bfloat16)],
+        scratch_shapes=[weights(count)],
         compiler_params=PARAMS,
+        cost_estimate=cost(count),
         name="hist",
-    )(got, own, predictions)
+    )(*operands, own)
     spread = lax.all_to_all(best, "rows", 0, 0, tiled=True)
     best_gain = jnp.max(spread, axis=(0, 1))[:NODES]
     return gains, best_gain, leaf_values, new_predictions

time: 61.2 us -> 58.8 us (0.961)
  blocking collectives: 46.5 us -> 10.1 us
  starting transfers between devices: 0 us -> 25.6 us
  waiting for transfers between devices: 0 us -> 6.32 us
  Pallas kernels: 13.3 us -> 14.4 us
  local copies, waits for them, and re-layouts: 0.01 us -> 0.9 us
    all_to_all x1 -> x0, blocking collectives: 37.1 us -> none  [body(): got = lax.all_to_all(pay, 'rows', 0, 0, tiled=True)]
    ppermute x0 -> x15, starting transfers between devices: none -> 25.6 us  [body(): lax.ppermute(blocks[k], 'rows', [(i, i ^ k) for i in range(peers)])]
    ppermute x0 -> x15, waiting for transfers between devices: none -> 6.32 us  [body(): lax.ppermute(blocks[k], 'rows', [(i, i ^ k) for i in range(peers)])]
    pallas_call x2 -> x4, Pallas kernels: 13.3 us -> 14.4 us  [the longest x2 7.57 us: body(): pl.pallas_call(functools.partial(stage_kernel, chunks, len(group)), out_s...]
    unnamed x4 -> x10, local copies, waits for them, and re-layouts: 0.01 us -> 0.9 us
    all_to_all x1, blocking collectives: 9.44 us -> 10.1 us  [body(): spread = lax.all_to_all(best, 'rows', 0, 0, tiled=True)]
  transfers between devices with their start and end apart: 0 -> 15, of which waited for: 0 -> 6; matrix products, arithmetic and copies ran while one was open for 0% -> 0% of each run, Pallas kernels for 0% -> 13%
where the time goes in v3:
time: 58.8 us; the launch traced here: 58.6 us
  starting transfers between devices  25.6 us (44%)
  Pallas kernels  14.4 us (24%)
  blocking collectives  10.1 us (17%)
  waiting for transfers between devices  6.32 us (11%)
  local copies, waits for them, and re-layouts  0.9 us (2%)
  between operations  0.71 us (1%)
    ppermute x15, starting transfers between devices, body(): lax.ppermute(blocks[k], 'rows', [(i, i ^ k) for i in range(peers)])  25.6 us
    all_to_all x1, blocking collectives, body(): spread = lax.all_to_all(best, 'rows', 0, 0, tiled=True)  10.1 us
    pallas_call x2, Pallas kernels, body(): pl.pallas_call(functools.partial(stage_kernel, chunks, len(group)), out_s...  7.57 us
    ppermute x15, waiting for transfers between devices, body(): lax.ppermute(blocks[k], 'rows', [(i, i ^ k) for i in range(peers)])  6.32 us
    pallas_call x1, Pallas kernels, body(): pl.pallas_call(functools.partial(last_kernel, chunks, bool(hops)), out_sh...  3.97 us
    pallas_call x1, Pallas kernels, body(): pl.pallas_call(functools.partial(prep_kernel, peers), out_shape=[jax.Shap...  2.89 us
  transfers between devices with their start and end apart: 15, of which 6 were waited for; matrix products, arithmetic and copies ran while one was open for 0% of the time, Pallas kernels for 13%

profile of v3, /device:TPU:0, one launch (start us, length us, event | category | flops | bytes accessed | tf_op | source)
XLA Modules:
  0.0 58.6 jit_solution(6820037229694693268)
XLA Ops:
  0.6 2.9 %prep.1 = (f32[20,128]{1,0:T(8,128)}, f32[144,128]{1,0:T(8,128)}, f32[144,128]{1,0:T(8,128)}, f32[144,128]{1,0:T(8,128)}, f32[144,128]{1,0:T(8,128)}, /*index=5*...) custom-call(s32[512,512]{1,0:T(8,128)} %bins_hbm.1, ...), custom_call_target="tpu_custom_call" | custom-call | tf_op jit(solution)/shard_map/prep/pallas_call | solution.py:338
  3.5 5.5 %collective-permute-start.8 = (f32[144,128]{1,0:T(8,128)}, f32[144,128]{1,0:T(8,128)S(1)}, u32[]{:S(2)}, u32[]{:S(2)}) collective-permute-start(f32[144,128]{1,0:T(8,128)} %get-tuple-element.38), channel_id=1, source_target_pairs={{0,15},{1,14},{2,13},{3,12},{4,11},{5,10},{6,9},{7,8},{8,7},{9,6},... | collective-permute-start | bytes 221192 | tf_op jit(solution)/shard_map/ppermute | solution.py:361
  9.1 0.6 %collective-permute-start.9 = (f32[144,128]{1,0:T(8,128)}, f32[144,128]{1,0:T(8,128)S(1)}, u32[]{:S(2)}, u32[]{:S(2)}) collective-permute-start(f32[144,128]{1,0:T(8,128)} %get-tuple-element.39), channel_id=1, source_target_pairs={{0,14},{1,15},{2,12},{3,13},{4,10},{5,11},{6,8},{7,9},{8,6},{9,7},... | collective-permute-start | bytes 221192 | tf_op jit(solution)/shard_map/ppermute | solution.py:361
  9.7 3.1 %collective-permute-start.10 = (f32[144,128]{1,0:T(8,128)}, f32[144,128]{1,0:T(8,128)S(1)}, u32[]{:S(2)}, u32[]{:S(2)}) collective-permute-start(f32[144,128]{1,0:T(8,128)} %get-tuple-element.40), channel_id=1, source_target_pairs={{0,13},{1,12},{2,15},{3,14},{4,9},{5,8},{6,11},{7,10},{8,5},{9,4},... | collective-permute-start | bytes 221192 | tf_op jit(solution)/shard_map/ppermute | solution.py:361
  12.8 0.3 collective-permute-start.11
  13.2 0.9 %collective-permute-start.12 = (f32[144,128]{1,0:T(8,128)}, f32[144,128]{1,0:T(8,128)S(1)}, u32[]{:S(2)}, u32[]{:S(2)}) collective-permute-start(f32[144,128]{1,0:T(8,128)} %get-tuple-element.42), channel_id=1, source_target_pairs={{0,3},{1,2},{2,1},{3,0},{4,7},{5,6},{6,5},{7,4},{8,11},{9,10},{10,... | collective-permute-start | bytes 221192 | tf_op jit(solution)/shard_map/ppermute | solution.py:361
  14.1 0.0 collective-permute-done.8.refs_1_
  14.1 0.9 %collective-permute-start.13 = (f32[144,128]{1,0:T(8,128)}, f32[144,128]{1,0:T(8,128)S(1)}, u32[]{:S(2)}, u32[]{:S(2)}) collective-permute-start(f32[144,128]{1,0:T(8,128)} %get-tuple-element.43), channel_id=1, source_target_pairs={{0,2},{1,3},{2,0},{3,1},{4,6},{5,7},{6,4},{7,5},{8,10},{9,11},{10,... | collective-permute-start | bytes 221192 | tf_op jit(solution)/shard_map/ppermute | solution.py:361
  15.0 2.2 %collective-permute-done.9.refs_2_ = f32[144,128]{1,0:T(8,128)S(1)} collective-permute-done((f32[144,128]{1,0:T(8,128)}, f32[144,128]{1,0:T(8,128)S(1)}, u32[]{:S(2)}, u32[]{:S(2)}) %collective-permute-start.9) | collective-permute-done | bytes 73760 | tf_op jit(solution)/shard_map/ppermute | solution.py:361
  17.2 0.0 collective-permute-start.14
  17.2 0.0 collective-permute-done.10.refs_3_
  17.3 4.2 %collective-permute-start = (f32[144,128]{1,0:T(8,128)}, f32[144,128]{1,0:T(8,128)S(1)}, u32[]{:S(2)}, u32[]{:S(2)}) collective-permute-start(f32[144,128]{1,0:T(8,128)} %get-tuple-element.29), channel_id=1, source_target_pairs={{0,7},{1,6},{2,5},{3,4},{4,3},{5,2},{6,1},{7,0},{8,15},{9,14},{10,... | collective-permute-start | bytes 221192 | tf_op jit(solution)/shard_map/ppermute | solution.py:361
  21.4 0.0 collective-permute-done.11.refs_4_
  21.4 2.7 %collective-permute-start.4 = (f32[144,128]{1,0:T(8,128)}, f32[144,128]{1,0:T(8,128)S(1)}, u32[]{:S(2)}, u32[]{:S(2)}) collective-permute-start(f32[144,128]{1,0:T(8,128)} %get-tuple-element.33), channel_id=1, source_target_pairs={{0,11},{1,10},{2,9},{3,8},{4,15},{5,14},{6,13},{7,12},{8,3},{9,2},... | collective-permute-start | bytes 221192 | tf_op jit(solution)/shard_map/ppermute | solution.py:361
  24.1 0.0 collective-permute-done.12.refs_5_
  24.1 1.1 %collective-permute-start.5 = (f32[144,128]{1,0:T(8,128)}, f32[144,128]{1,0:T(8,128)S(1)}, u32[]{:S(2)}, u32[]{:S(2)}) collective-permute-start(f32[144,128]{1,0:T(8,128)} %get-tuple-element.34), channel_id=1, source_target_pairs={{0,10},{1,11},{2,8},{3,9},{4,14},{5,15},{6,12},{7,13},{8,2},{9,3},... | collective-permute-start | bytes 221192 | tf_op jit(solution)/shard_map/ppermute | solution.py:361
  25.2 0.0 collective-permute-done.13.refs_6_
  25.2 2.6 %collective-permute-start.6 = (f32[144,128]{1,0:T(8,128)}, f32[144,128]{1,0:T(8,128)S(1)}, u32[]{:S(2)}, u32[]{:S(2)}) collective-permute-start(f32[144,128]{1,0:T(8,128)} %get-tuple-element.35), channel_id=1, source_target_pairs={{0,9},{1,8},{2,11},{3,10},{4,13},{5,12},{6,15},{7,14},{8,1},{9,0},... | collective-permute-start | bytes 221192 | tf_op jit(solution)/shard_map/ppermute | solution.py:361
  27.7 0.0 collective-permute-done.14.refs_7_
  27.7 0.3 collective-permute-start.7
  28.1 0.0 copy-start
  28.1 0.9 %copy-done = f32[144,128]{1,0:T(8,128)S(1)} copy-done((f32[144,128]{1,0:T(8,128)S(1)}, f32[144,128]{1,0:T(8,128)}, u32[]{:S(2)}) %copy-start) | copy-done | bytes 73752
  29.0 0.0 copy-start.4
  29.0 0.0 copy-start.3
  29.0 0.0 copy-start.2
  29.0 4.9 %shard_map.102 = (f32[32,64,128]{2,1,0:T(8,128)S(1)}, f32[4,16,128]{2,1,0:T(8,128)S(1)}) custom-call(f32[144,128]{1,0:T(8,128)S(1)} %copy-done, f32[144,128]{1,0:T(8,128)S(1)} %collective-permute-done.8.refs_1_, f32[144,128]{1,0:T(8,128)S(1)} %collective-permute-done.9.refs_2_, f32[144,128]{1,0:T(8,128)S(1)} %collective-permute-done.10.refs_3_, ...), custom_call_target="tpu_custom_call" | custom-call | flops 2147483648 | bytes 524288 | tf_op jit(solution)/shard_map/pallas_call | solution.py:367
  33.8 0.0 collective-permute-done.4.refs_0_
  33.9 0.0 copy-done.4
  33.9 1.6 %collective-permute-start.1 = (f32[144,128]{1,0:T(8,128)S(1)}, f32[144,128]{1,0:T(8,128)S(1)}, u32[]{:S(2)}, u32[]{:S(2)}) collective-permute-start(f32[144,128]{1,0:T(8,128)S(1)} %copy-done.4), channel_id=1, source_target_pairs={{0,6},{1,7},{2,4},{3,5},{4,2},{5,3},{6,0},{7,1},{8,14},{9,15},{10,... | collective-permute-start | bytes 221192 | tf_op jit(solution)/shard_map/ppermute | solution.py:361
  35.5 0.5 collective-permute-done.5.refs_1_
  36.0 0.0 copy-done.3
  36.0 1.0 %collective-permute-start.2 = (f32[144,128]{1,0:T(8,128)S(1)}, f32[144,128]{1,0:T(8,128)S(1)}, u32[]{:S(2)}, u32[]{:S(2)}) collective-permute-start(f32[144,128]{1,0:T(8,128)S(1)} %copy-done.3), channel_id=1, source_target_pairs={{0,5},{1,4},{2,7},{3,6},{4,1},{5,0},{6,3},{7,2},{8,13},{9,12},{10,... | collective-permute-start | bytes 221192 | tf_op jit(solution)/shard_map/ppermute | solution.py:361
  37.0 0.1 collective-permute-done.6.refs_2_
  37.2 0.0 copy-done.2
  37.2 0.7 %collective-permute-start.3 = (f32[144,128]{1,0:T(8,128)S(1)}, f32[144,128]{1,0:T(8,128)S(1)}, u32[]{:S(2)}, u32[]{:S(2)}) collective-permute-start(f32[144,128]{1,0:T(8,128)S(1)} %copy-done.2), channel_id=1, source_target_pairs={{0,4},{1,5},{2,6},{3,7},{4,0},{5,1},{6,2},{7,3},{8,12},{9,13},{10,... | collective-permute-start | bytes 221192 | tf_op jit(solution)/shard_map/ppermute | solution.py:361
  37.8 1.5 %collective-permute-done.7.refs_3_ = f32[144,128]{1,0:T(8,128)S(1)} collective-permute-done((f32[144,128]{1,0:T(8,128)}, f32[144,128]{1,0:T(8,128)S(1)}, u32[]{:S(2)}, u32[]{:S(2)}) %collective-permute-start.7) | collective-permute-done | bytes 73760 | tf_op jit(solution)/shard_map/ppermute | solution.py:361
  39.3 0.0 copy-start.1
  39.3 2.7 %shard_map.103 = (f32[32,64,128]{2,1,0:T(8,128)S(1)}, f32[4,16,128]{2,1,0:T(8,128)S(1)}) custom-call(f32[144,128]{1,0:T(8,128)S(1)} %collective-permute-done.4.refs_0_, f32[144,128]{1,0:T(8,128)S(1)} %collective-permute-done.5.refs_1_, f32[144,128]{1,0:T(8,128)S(1)} %collective-permute-done.6.refs_2_, f32[144,128]{1,0:T(8,128)S(1)} %collective-permute-done.7.refs_3_, ...), custom_call_target="tpu_custom_call" | custom-call | flops 1073741824 | bytes 262144 | tf_op jit(solution)/shard_map/pallas_call | solution.py:367
  42.0 0.0 collective-permute-done.refs_0_
  42.0 0.0 collective-permute-done.1.refs_1_
  42.0 0.3 collective-permute-done.2.refs_2_
  42.4 1.6 %collective-permute-done.3.refs_3_ = f32[144,128]{1,0:T(8,128)S(1)} collective-permute-done((f32[144,128]{1,0:T(8,128)S(1)}, f32[144,128]{1,0:T(8,128)S(1)}, u32[]{:S(2)}, u32[]{:S(2)}) %collective-permute-start.3) | collective-permute-done | bytes 73760 | tf_op jit(solution)/shard_map/ppermute | solution.py:361
  44.0 0.0 copy-done.1
  44.0 4.0 %hist.1 = (f32[32,16,256]{2,1,0:T(8,128)}, f32[16,1,128]{2,1,0:T(1,128)S(1)}, f32[2,16]{1,0:T(2,128)}, f32[512]{0:T(512)}) custom-call(f32[144,128]{1,0:T(8,128)S(1)} %collective-permute-done.refs_0_, f32[144,128]{1,0:T(8,128)S(1)} %collective-permute-done.1.refs_1_, f32[144,128]{1,0:T(8,128)S(1)} %collective-permute-done.2.refs_2_, ...), custom_call_target="tpu_custom_call" | custom-call | flops 1073741824 | bytes 262144 | tf_op jit(solution)/shard_map/hist/pallas_call | solution.py:384
  47.9 10.1 %all_to_all.5 = f32[16,1,128]{2,1,0:T(1,128)S(1)} all-to-all(f32[16,1,128]{2,1,0:T(1,128)S(1)} %get-tuple-element.51), channel_id=1, replica_groups=mesh['groups'=2,'rows'=16] {'rows'}, dimensions={0} | all-to-all | bytes 16384 | tf_op jit(solution)/shard_map/all_to_all | solution.py:399
  58.0 0.5 reduce_max.9
Async XLA Ops:
  3.5 10.6 %collective-permute-start.8 = (f32[144,128]{1,0:T(8,128)}, f32[144,128]{1,0:T(8,128)S(1)}, u32[]{:S(2)}, u32[]{:S(2)}) collective-permute-start(f32[144,128]{1,0:T(8,128)} %get-tuple-element.38), channel_id=1, source_target_pairs={{0,15},{1,14},{2,13},{3,12},{4,11},{5,10},{6,9},{7,8},{8,7},{9,6},... | collective-permute-start | bytes 221192 | tf_op jit(solution)/shard_map/ppermute | solution.py:361
  9.1 8.1 %collective-permute-start.9 = (f32[144,128]{1,0:T(8,128)}, f32[144,128]{1,0:T(8,128)S(1)}, u32[]{:S(2)}, u32[]{:S(2)}) collective-permute-start(f32[144,128]{1,0:T(8,128)} %get-tuple-element.39), channel_id=1, source_target_pairs={{0,14},{1,15},{2,12},{3,13},{4,10},{5,11},{6,8},{7,9},{8,6},{9,7},... | collective-permute-start | bytes 221192 | tf_op jit(solution)/shard_map/ppermute | solution.py:361
  9.7 7.5 %collective-permute-start.10 = (f32[144,128]{1,0:T(8,128)}, f32[144,128]{1,0:T(8,128)S(1)}, u32[]{:S(2)}, u32[]{:S(2)}) collective-permute-start(f32[144,128]{1,0:T(8,128)} %get-tuple-element.40), channel_id=1, source_target_pairs={{0,13},{1,12},{2,15},{3,14},{4,9},{5,8},{6,11},{7,10},{8,5},{9,4},... | collective-permute-start | bytes 221192 | tf_op jit(solution)/shard_map/ppermute | solution.py:361
  12.8 8.6 %collective-permute-start.11 = (f32[144,128]{1,0:T(8,128)}, f32[144,128]{1,0:T(8,128)S(1)}, u32[]{:S(2)}, u32[]{:S(2)}) collective-permute-start(f32[144,128]{1,0:T(8,128)} %get-tuple-element.41), channel_id=1, source_target_pairs={{0,12},{1,13},{2,14},{3,15},{4,8},{5,9},{6,10},{7,11},{8,4},{9,5},... | collective-permute-start | bytes 221192 | tf_op jit(solution)/shard_map/ppermute | solution.py:361
  13.2 10.9 %collective-permute-start.12 = (f32[144,128]{1,0:T(8,128)}, f32[144,128]{1,0:T(8,128)S(1)}, u32[]{:S(2)}, u32[]{:S(2)}) collective-permute-start(f32[144,128]{1,0:T(8,128)} %get-tuple-element.42), channel_id=1, source_target_pairs={{0,3},{1,2},{2,1},{3,0},{4,7},{5,6},{6,5},{7,4},{8,11},{9,10},{10,... | collective-permute-start | bytes 221192 | tf_op jit(solution)/shard_map/ppermute | solution.py:361
  14.1 11.1 %collective-permute-start.13 = (f32[144,128]{1,0:T(8,128)}, f32[144,128]{1,0:T(8,128)S(1)}, u32[]{:S(2)}, u32[]{:S(2)}) collective-permute-start(f32[144,128]{1,0:T(8,128)} %get-tuple-element.43), channel_id=1, source_target_pairs={{0,2},{1,3},{2,0},{3,1},{4,6},{5,7},{6,4},{7,5},{8,10},{9,11},{10,... | collective-permute-start | bytes 221192 | tf_op jit(solution)/shard_map/ppermute | solution.py:361
  17.2 10.5 %collective-permute-start.14 = (f32[144,128]{1,0:T(8,128)}, f32[144,128]{1,0:T(8,128)S(1)}, u32[]{:S(2)}, u32[]{:S(2)}) collective-permute-start(f32[144,128]{1,0:T(8,128)} %get-tuple-element.44), channel_id=1, source_target_pairs={{0,1},{1,0},{2,3},{3,2},{4,5},{5,4},{6,7},{7,6},{8,9},{9,8},{10,11... | collective-permute-start | bytes 221192 | tf_op jit(solution)/shard_map/ppermute | solution.py:361
  17.3 24.8 %collective-permute-start = (f32[144,128]{1,0:T(8,128)}, f32[144,128]{1,0:T(8,128)S(1)}, u32[]{:S(2)}, u32[]{:S(2)}) collective-permute-start(f32[144,128]{1,0:T(8,128)} %get-tuple-element.29), channel_id=1, source_target_pairs={{0,7},{1,6},{2,5},{3,4},{4,3},{5,2},{6,1},{7,0},{8,15},{9,14},{10,... | collective-permute-start | bytes 221192 | tf_op jit(solution)/shard_map/ppermute | solution.py:361
  21.4 12.4 %collective-permute-start.4 = (f32[144,128]{1,0:T(8,128)}, f32[144,128]{1,0:T(8,128)S(1)}, u32[]{:S(2)}, u32[]{:S(2)}) collective-permute-start(f32[144,128]{1,0:T(8,128)} %get-tuple-element.33), channel_id=1, source_target_pairs={{0,11},{1,10},{2,9},{3,8},{4,15},{5,14},{6,13},{7,12},{8,3},{9,2},... | collective-permute-start | bytes 221192 | tf_op jit(solution)/shard_map/ppermute | solution.py:361
  24.1 11.9 %collective-permute-start.5 = (f32[144,128]{1,0:T(8,128)}, f32[144,128]{1,0:T(8,128)S(1)}, u32[]{:S(2)}, u32[]{:S(2)}) collective-permute-start(f32[144,128]{1,0:T(8,128)} %get-tuple-element.34), channel_id=1, source_target_pairs={{0,10},{1,11},{2,8},{3,9},{4,14},{5,15},{6,12},{7,13},{8,2},{9,3},... | collective-permute-start | bytes 221192 | tf_op jit(solution)/shard_map/ppermute | solution.py:361
  25.2 12.0 %collective-permute-start.6 = (f32[144,128]{1,0:T(8,128)}, f32[144,128]{1,0:T(8,128)S(1)}, u32[]{:S(2)}, u32[]{:S(2)}) collective-permute-start(f32[144,128]{1,0:T(8,128)} %get-tuple-element.35), channel_id=1, source_target_pairs={{0,9},{1,8},{2,11},{3,10},{4,13},{5,12},{6,15},{7,14},{8,1},{9,0},... | collective-permute-start | bytes 221192 | tf_op jit(solution)/shard_map/ppermute | solution.py:361
  27.7 11.6 %collective-permute-start.7 = (f32[144,128]{1,0:T(8,128)}, f32[144,128]{1,0:T(8,128)S(1)}, u32[]{:S(2)}, u32[]{:S(2)}) collective-permute-start(f32[144,128]{1,0:T(8,128)} %get-tuple-element.36), channel_id=1, source_target_pairs={{0,8},{1,9},{2,10},{3,11},{4,12},{5,13},{6,14},{7,15},{8,0},{9,1},... | collective-permute-start | bytes 221192 | tf_op jit(solution)/shard_map/ppermute | solution.py:361
  28.1 0.9 %copy-start = (f32[144,128]{1,0:T(8,128)S(1)}, f32[144,128]{1,0:T(8,128)}, u32[]{:S(2)}) copy-start(f32[144,128]{1,0:T(8,128)} %get-tuple-element.37.refs_0_) | copy-start | bytes 221188
  29.0 4.9 %copy-start.4 = (f32[144,128]{1,0:T(8,128)S(1)}, f32[144,128]{1,0:T(8,128)}, u32[]{:S(2)}) copy-start(f32[144,128]{1,0:T(8,128)} %get-tuple-element.30) | copy-start | bytes 221188
  29.0 7.0 %copy-start.3 = (f32[144,128]{1,0:T(8,128)S(1)}, f32[144,128]{1,0:T(8,128)}, u32[]{:S(2)}) copy-start(f32[144,128]{1,0:T(8,128)} %get-tuple-element.31) | copy-start | bytes 221188
  29.0 8.2 %copy-start.2 = (f32[144,128]{1,0:T(8,128)S(1)}, f32[144,128]{1,0:T(8,128)}, u32[]{:S(2)}) copy-start(f32[144,128]{1,0:T(8,128)} %get-tuple-element.32) | copy-start | bytes 221188
  33.9 8.2 %collective-permute-start.1 = (f32[144,128]{1,0:T(8,128)S(1)}, f32[144,128]{1,0:T(8,128)S(1)}, u32[]{:S(2)}, u32[]{:S(2)}) collective-permute-start(f32[144,128]{1,0:T(8,128)S(1)} %copy-done.4), channel_id=1, source_target_pairs={{0,6},{1,7},{2,4},{3,5},{4,2},{5,3},{6,0},{7,1},{8,14},{9,15},{10,... | collective-permute-start | bytes 221192 | tf_op jit(solution)/shard_map/ppermute | solution.py:361
  36.0 6.4 %collective-permute-start.2 = (f32[144,128]{1,0:T(8,128)S(1)}, f32[144,128]{1,0:T(8,128)S(1)}, u32[]{:S(2)}, u32[]{:S(2)}) collective-permute-start(f32[144,128]{1,0:T(8,128)S(1)} %copy-done.3), channel_id=1, source_target_pairs={{0,5},{1,4},{2,7},{3,6},{4,1},{5,0},{6,3},{7,2},{8,13},{9,12},{10,... | collective-permute-start | bytes 221192 | tf_op jit(solution)/shard_map/ppermute | solution.py:361
  37.2 6.8 %collective-permute-start.3 = (f32[144,128]{1,0:T(8,128)S(1)}, f32[144,128]{1,0:T(8,128)S(1)}, u32[]{:S(2)}, u32[]{:S(2)}) collective-permute-start(f32[144,128]{1,0:T(8,128)S(1)} %copy-done.2), channel_id=1, source_target_pairs={{0,4},{1,5},{2,6},{3,7},{4,0},{5,1},{6,2},{7,3},{8,12},{9,13},{10,... | collective-permute-start | bytes 221192 | tf_op jit(solution)/shard_map/ppermute | solution.py:361
  39.3 4.6 %copy-start.1 = (f32[20,128]{1,0:T(8,128)S(1)}, f32[20,128]{1,0:T(8,128)}, u32[]{:S(2)}) copy-start(f32[20,128]{1,0:T(8,128)} %get-tuple-element.49.refs_6_) | copy-start | bytes 30724

commit v4 on v3

--- a/solution.py
+++ b/solution.py
@@ -29,13 +29,13 @@
     far = list(range(peers - 1, peers // 2 - 1, -1))
     near = list(range(peers // 2 - 1, 0, -1))
     split = max(len(near) - 3, 0)
-    return far[:4] + near[split:] + far[4:] + near[:split]
+    return far[:4] + near[split:] + far[4:5] + near[:split] + far[5:]
 
 
 def stage_hops(peers):
     order = [0] + hop_order(peers)
-    half, quarter = peers // 2, peers // 4
-    return [order[:half], order[half : half + quarter], order[half + quarter :]]
+    early, late = peers // 2, max(peers * 13 // 16, peers // 2 + 1)
+    return [order[:early], order[early:late], order[late:]]
 
 
 def prep_kernel(peers, bins_hbm, *refs):
@@ -170,7 +170,7 @@
     f8, i16 = jnp.float8_e4m3fn, jnp.int16
     block = min(count, BLOCK)
     quads = owned // QUAD
-    group = min(4, quads)
+    group = min(quads, 8 if count <= 4 else 4)
     spot = lax.broadcasted_iota(jnp.int32, (32, LANES), 0)
     steps = [(spot + 32 * i).astype(i16) for i in range(HALF // 32)]
     one = jnp.ones((32, LANES), f8)
@@ -235,6 +235,8 @@
 
         for a in acc:
             pltpu.matmul_pop(a)
+        if quads == group:
+            return step(0, carry)
         return lax.fori_loop(0, quads // group, step, carry)
 
     shape = ((4 * 2 * NODES, BINS), jnp.float32)
@@ -284,7 +286,6 @@
     read = reader(block_refs)
     count = len(block_refs) if len(block_refs) > 1 else peers
     sums = weigh_all(read, count, chunks * owned, chunks, w_ref, sums)
-    settle(sums, chunks, own_ref, leaf_ref, new_ref)
 
     def finish(q, acc, best):
         for m in range(2):
@@ -310,6 +311,7 @@
 
     least = jnp.full((NODES, BINS), -jnp.inf, jnp.float32)
     best = sweep(read, count, w_ref, owned, chunks, finish, least)
+    settle(sums, chunks, own_ref, leaf_ref, new_ref)
     best = jnp.maximum(best[:, :LANES], best[:, LANES:])
     best = jnp.concatenate([best, jnp.zeros((LANES - NODES, LANES), jnp.float32)], axis=0)
     row = jnp.max(best.T, axis=0, keepdims=True)

time: 58.8 us -> 59.8 us (1.017)
  waiting for transfers between devices: 6.32 us -> 8.81 us
  blocking collectives: 10.1 us -> 9.31 us
    ppermute x15, waiting for transfers between devices: 6.32 us -> 8.81 us  [body(): lax.ppermute(blocks[k], 'rows', [(i, i ^ k) for i in range(peers)])]
    pallas_call x1, Pallas kernels: 3.97 us -> 2.86 us  [body(): pl.pallas_call(functools.partial(last_kernel, chunks, bool(hops)), out_sh...]
    all_to_all x1, blocking collectives: 10.1 us -> 9.31 us  [body(): spread = lax.all_to_all(best, 'rows', 0, 0, tiled=True)]
  transfers between devices with their start and end apart: 15 -> 15, of which waited for: 6 -> 4; matrix products, arithmetic and copies ran while one was open for 0% -> 0% of each run, Pallas kernels for 13% -> 14%
where the time goes in v4:
time: 59.8 us; the launch traced here: 59.6 us
  starting transfers between devices  25.4 us (42%)
  Pallas kernels  13.9 us (23%)
  blocking collectives  9.31 us (16%)
  waiting for transfers between devices  8.81 us (15%)
  local copies, waits for them, and re-layouts  0.9 us (2%)
  between operations  0.7 us (1%)
    ppermute x15, starting transfers between devices, body(): lax.ppermute(blocks[k], 'rows', [(i, i ^ k) for i in range(peers)])  25.4 us
    all_to_all x1, blocking collectives, body(): spread = lax.all_to_all(best, 'rows', 0, 0, tiled=True)  9.31 us
    ppermute x15, waiting for transfers between devices, body(): lax.ppermute(blocks[k], 'rows', [(i, i ^ k) for i in range(peers)])  8.81 us
    pallas_call x2, Pallas kernels, body(): pl.pallas_call(functools.partial(stage_kernel, chunks, len(group)), out_s...  8.13 us
    pallas_call x1, Pallas kernels, body(): pl.pallas_call(functools.partial(prep_kernel, peers), out_shape=[jax.Shap...  2.89 us
    pallas_call x1, Pallas kernels, body(): pl.pallas_call(functools.partial(last_kernel, chunks, bool(hops)), out_sh...  2.86 us
  transfers between devices with their start and end apart: 15, of which 4 were waited for; matrix products, arithmetic and copies ran while one was open for 0% of the time, Pallas kernels for 14%

profile of v4, /device:TPU:0, one launch (start us, length us, event | category | flops | bytes accessed | tf_op | source)
XLA Modules:
  0.0 59.6 jit_solution(698881457248872569)
XLA Ops:
  0.6 2.9 %prep.1 = (f32[20,128]{1,0:T(8,128)}, f32[144,128]{1,0:T(8,128)}, f32[144,128]{1,0:T(8,128)}, f32[144,128]{1,0:T(8,128)}, f32[144,128]{1,0:T(8,128)}, /*index=5*...) custom-call(s32[512,512]{1,0:T(8,128)} %bins_hbm.1, ...), custom_call_target="tpu_custom_call" | custom-call | tf_op jit(solution)/shard_map/prep/pallas_call | solution.py:340
  3.5 5.5 %collective-permute-start.8 = (f32[144,128]{1,0:T(8,128)}, f32[144,128]{1,0:T(8,128)S(1)}, u32[]{:S(2)}, u32[]{:S(2)}) collective-permute-start(f32[144,128]{1,0:T(8,128)} %get-tuple-element.38), channel_id=1, source_target_pairs={{0,15},{1,14},{2,13},{3,12},{4,11},{5,10},{6,9},{7,8},{8,7},{9,6},... | collective-permute-start | bytes 221192 | tf_op jit(solution)/shard_map/ppermute | solution.py:363
  9.1 0.6 %collective-permute-start.9 = (f32[144,128]{1,0:T(8,128)}, f32[144,128]{1,0:T(8,128)S(1)}, u32[]{:S(2)}, u32[]{:S(2)}) collective-permute-start(f32[144,128]{1,0:T(8,128)} %get-tuple-element.39), channel_id=1, source_target_pairs={{0,14},{1,15},{2,12},{3,13},{4,10},{5,11},{6,8},{7,9},{8,6},{9,7},... | collective-permute-start | bytes 221192 | tf_op jit(solution)/shard_map/ppermute | solution.py:363
  9.7 3.1 %collective-permute-start.10 = (f32[144,128]{1,0:T(8,128)}, f32[144,128]{1,0:T(8,128)S(1)}, u32[]{:S(2)}, u32[]{:S(2)}) collective-permute-start(f32[144,128]{1,0:T(8,128)} %get-tuple-element.40), channel_id=1, source_target_pairs={{0,13},{1,12},{2,15},{3,14},{4,9},{5,8},{6,11},{7,10},{8,5},{9,4},... | collective-permute-start | bytes 221192 | tf_op jit(solution)/shard_map/ppermute | solution.py:363
  12.8 0.3 collective-permute-start.11
  13.2 0.9 %collective-permute-start.12 = (f32[144,128]{1,0:T(8,128)}, f32[144,128]{1,0:T(8,128)S(1)}, u32[]{:S(2)}, u32[]{:S(2)}) collective-permute-start(f32[144,128]{1,0:T(8,128)} %get-tuple-element.42), channel_id=1, source_target_pairs={{0,3},{1,2},{2,1},{3,0},{4,7},{5,6},{6,5},{7,4},{8,11},{9,10},{10,... | collective-permute-start | bytes 221192 | tf_op jit(solution)/shard_map/ppermute | solution.py:363
  14.1 0.0 collective-permute-done.8.refs_1_
  14.1 0.9 %collective-permute-start.13 = (f32[144,128]{1,0:T(8,128)}, f32[144,128]{1,0:T(8,128)S(1)}, u32[]{:S(2)}, u32[]{:S(2)}) collective-permute-start(f32[144,128]{1,0:T(8,128)} %get-tuple-element.43), channel_id=1, source_target_pairs={{0,2},{1,3},{2,0},{3,1},{4,6},{5,7},{6,4},{7,5},{8,10},{9,11},{10,... | collective-permute-start | bytes 221192 | tf_op jit(solution)/shard_map/ppermute | solution.py:363
  15.0 2.2 %collective-permute-done.9.refs_2_ = f32[144,128]{1,0:T(8,128)S(1)} collective-permute-done((f32[144,128]{1,0:T(8,128)}, f32[144,128]{1,0:T(8,128)S(1)}, u32[]{:S(2)}, u32[]{:S(2)}) %collective-permute-start.9) | collective-permute-done | bytes 73760 | tf_op jit(solution)/shard_map/ppermute | solution.py:363
  17.2 0.0 collective-permute-start.14
  17.2 0.0 collective-permute-done.10.refs_3_
  17.3 5.3 %collective-permute-start.3 = (f32[144,128]{1,0:T(8,128)}, f32[144,128]{1,0:T(8,128)S(1)}, u32[]{:S(2)}, u32[]{:S(2)}) collective-permute-start(f32[144,128]{1,0:T(8,128)} %get-tuple-element.32), channel_id=1, source_target_pairs={{0,11},{1,10},{2,9},{3,8},{4,15},{5,14},{6,13},{7,12},{8,3},{9,2},... | collective-permute-start | bytes 221192 | tf_op jit(solution)/shard_map/ppermute | solution.py:363
  22.5 0.0 collective-permute-done.11.refs_4_
  22.5 0.4 collective-permute-start.4
  22.9 0.0 collective-permute-done.12.refs_5_
  22.9 2.5 %collective-permute-start.5 = (f32[144,128]{1,0:T(8,128)}, f32[144,128]{1,0:T(8,128)S(1)}, u32[]{:S(2)}, u32[]{:S(2)}) collective-permute-start(f32[144,128]{1,0:T(8,128)} %get-tuple-element.34), channel_id=1, source_target_pairs={{0,6},{1,7},{2,4},{3,5},{4,2},{5,3},{6,0},{7,1},{8,14},{9,15},{10,... | collective-permute-start | bytes 221192 | tf_op jit(solution)/shard_map/ppermute | solution.py:363
  25.5 0.0 collective-permute-done.13.refs_6_
  25.5 0.4 collective-permute-start.6
  25.8 0.0 collective-permute-done.14.refs_7_
  25.8 1.1 %collective-permute-start.7 = (f32[144,128]{1,0:T(8,128)}, f32[144,128]{1,0:T(8,128)S(1)}, u32[]{:S(2)}, u32[]{:S(2)}) collective-permute-start(f32[144,128]{1,0:T(8,128)} %get-tuple-element.36), channel_id=1, source_target_pairs={{0,4},{1,5},{2,6},{3,7},{4,0},{5,1},{6,2},{7,3},{8,12},{9,13},{10,... | collective-permute-start | bytes 221192 | tf_op jit(solution)/shard_map/ppermute | solution.py:363
  26.9 0.0 copy-start
  26.9 0.9 %copy-done = f32[144,128]{1,0:T(8,128)S(1)} copy-done((f32[144,128]{1,0:T(8,128)S(1)}, f32[144,128]{1,0:T(8,128)}, u32[]{:S(2)}) %copy-start) | copy-done | bytes 73752
  27.8 0.0 copy-start.4
  27.8 0.0 copy-start.3
  27.8 0.0 copy-start.2
  27.8 4.9 %shard_map.102 = (f32[32,64,128]{2,1,0:T(8,128)S(1)}, f32[4,16,128]{2,1,0:T(8,128)S(1)}) custom-call(f32[144,128]{1,0:T(8,128)S(1)} %copy-done, f32[144,128]{1,0:T(8,128)S(1)} %collective-permute-done.8.refs_1_, f32[144,128]{1,0:T(8,128)S(1)} %collective-permute-done.9.refs_2_, f32[144,128]{1,0:T(8,128)S(1)} %collective-permute-done.10.refs_3_, ...), custom_call_target="tpu_custom_call" | custom-call | flops 2147483648 | bytes 524288 | tf_op jit(solution)/shard_map/pallas_call | solution.py:369
  32.7 0.0 collective-permute-done.3.refs_0_
  32.7 0.0 copy-done.4
  32.7 1.9 %collective-permute-start = (f32[144,128]{1,0:T(8,128)S(1)}, f32[144,128]{1,0:T(8,128)S(1)}, u32[]{:S(2)}, u32[]{:S(2)}) collective-permute-start(f32[144,128]{1,0:T(8,128)S(1)} %copy-done.4), channel_id=1, source_target_pairs={{0,10},{1,11},{2,8},{3,9},{4,14},{5,15},{6,12},{7,13},{8,2},{9,3},... | collective-permute-start | bytes 221192 | tf_op jit(solution)/shard_map/ppermute | solution.py:363
  34.7 0.0 collective-permute-done.4.refs_1_
  34.7 0.0 copy-done.3
  34.7 1.7 %collective-permute-start.1 = (f32[144,128]{1,0:T(8,128)S(1)}, f32[144,128]{1,0:T(8,128)S(1)}, u32[]{:S(2)}, u32[]{:S(2)}) collective-permute-start(f32[144,128]{1,0:T(8,128)S(1)} %copy-done.3), channel_id=1, source_target_pairs={{0,9},{1,8},{2,11},{3,10},{4,13},{5,12},{6,15},{7,14},{8,1},{9,0},... | collective-permute-start | bytes 221192 | tf_op jit(solution)/shard_map/ppermute | solution.py:363
  36.4 0.0 collective-permute-done.5.refs_2_
  36.4 0.0 copy-done.2
  36.4 0.6 %collective-permute-start.2 = (f32[144,128]{1,0:T(8,128)S(1)}, f32[144,128]{1,0:T(8,128)S(1)}, u32[]{:S(2)}, u32[]{:S(2)}) collective-permute-start(f32[144,128]{1,0:T(8,128)S(1)} %copy-done.2), channel_id=1, source_target_pairs={{0,8},{1,9},{2,10},{3,11},{4,12},{5,13},{6,14},{7,15},{8,0},{9,1},... | collective-permute-start | bytes 221192 | tf_op jit(solution)/shard_map/ppermute | solution.py:363
  37.0 0.0 collective-permute-done.6.refs_3_
  37.0 0.0 collective-permute-done.7.refs_4_
  37.0 0.0 copy-start.1
  37.0 3.2 %shard_map.103 = (f32[32,64,128]{2,1,0:T(8,128)S(1)}, f32[4,16,128]{2,1,0:T(8,128)S(1)}) custom-call(f32[144,128]{1,0:T(8,128)S(1)} %collective-permute-done.3.refs_0_, f32[144,128]{1,0:T(8,128)S(1)} %collective-permute-done.4.refs_1_, f32[144,128]{1,0:T(8,128)S(1)} %collective-permute-done.5.refs_2_, f32[144,128]{1,0:T(8,128)S(1)} %collective-permute-done.6.refs_3_, ...), custom_call_target="tpu_custom_call" | custom-call | flops 1342177280 | bytes 327680 | tf_op jit(solution)/shard_map/pallas_call | solution.py:369
  40.3 3.8 %collective-permute-done.refs_0_ = f32[144,128]{1,0:T(8,128)S(1)} collective-permute-done((f32[144,128]{1,0:T(8,128)S(1)}, f32[144,128]{1,0:T(8,128)S(1)}, u32[]{:S(2)}, u32[]{:S(2)}) %collective-permute-start) | collective-permute-done | bytes 73760 | tf_op jit(solution)/shard_map/ppermute | solution.py:363
  44.1 1.1 %collective-permute-done.1.refs_1_ = f32[144,128]{1,0:T(8,128)S(1)} collective-permute-done((f32[144,128]{1,0:T(8,128)S(1)}, f32[144,128]{1,0:T(8,128)S(1)}, u32[]{:S(2)}, u32[]{:S(2)}) %collective-permute-start.1) | collective-permute-done | bytes 73760 | tf_op jit(solution)/shard_map/ppermute | solution.py:363
  45.2 1.6 %collective-permute-done.2.refs_2_ = f32[144,128]{1,0:T(8,128)S(1)} collective-permute-done((f32[144,128]{1,0:T(8,128)S(1)}, f32[144,128]{1,0:T(8,128)S(1)}, u32[]{:S(2)}, u32[]{:S(2)}) %collective-permute-start.2) | collective-permute-done | bytes 73760 | tf_op jit(solution)/shard_map/ppermute | solution.py:363
  46.8 0.0 copy-done.1
  46.8 2.9 %hist.1 = (f32[32,16,256]{2,1,0:T(8,128)}, f32[16,1,128]{2,1,0:T(1,128)S(1)}, f32[2,16]{1,0:T(2,128)}, f32[512]{0:T(512)}) custom-call(f32[144,128]{1,0:T(8,128)S(1)} %collective-permute-done.refs_0_, f32[144,128]{1,0:T(8,128)S(1)} %collective-permute-done.1.refs_1_, f32[144,128]{1,0:T(8,128)S(1)} %collective-permute-done.2.refs_2_, ...), custom_call_target="tpu_custom_call" | custom-call | flops 805306368 | bytes 196608 | tf_op jit(solution)/shard_map/hist/pallas_call | solution.py:386
  49.7 9.3 %all_to_all.5 = f32[16,1,128]{2,1,0:T(1,128)S(1)} all-to-all(f32[16,1,128]{2,1,0:T(1,128)S(1)} %get-tuple-element.51), channel_id=1, replica_groups=mesh['groups'=2,'rows'=16] {'rows'}, dimensions={0} | all-to-all | bytes 16384 | tf_op jit(solution)/shard_map/all_to_all | solution.py:401
  59.0 0.5 reduce_max.9
Async XLA Ops:
  3.5 10.6 %collective-permute-start.8 = (f32[144,128]{1,0:T(8,128)}, f32[144,128]{1,0:T(8,128)S(1)}, u32[]{:S(2)}, u32[]{:S(2)}) collective-permute-start(f32[144,128]{1,0:T(8,128)} %get-tuple-element.38), channel_id=1, source_target_pairs={{0,15},{1,14},{2,13},{3,12},{4,11},{5,10},{6,9},{7,8},{8,7},{9,6},... | collective-permute-start | bytes 221192 | tf_op jit(solution)/shard_map/ppermute | solution.py:363
  9.1 8.1 %collective-permute-start.9 = (f32[144,128]{1,0:T(8,128)}, f32[144,128]{1,0:T(8,128)S(1)}, u32[]{:S(2)}, u32[]{:S(2)}) collective-permute-start(f32[144,128]{1,0:T(8,128)} %get-tuple-element.39), channel_id=1, source_target_pairs={{0,14},{1,15},{2,12},{3,13},{4,10},{5,11},{6,8},{7,9},{8,6},{9,7},... | collective-permute-start | bytes 221192 | tf_op jit(solution)/shard_map/ppermute | solution.py:363
  9.7 7.5 %collective-permute-start.10 = (f32[144,128]{1,0:T(8,128)}, f32[144,128]{1,0:T(8,128)S(1)}, u32[]{:S(2)}, u32[]{:S(2)}) collective-permute-start(f32[144,128]{1,0:T(8,128)} %get-tuple-element.40), channel_id=1, source_target_pairs={{0,13},{1,12},{2,15},{3,14},{4,9},{5,8},{6,11},{7,10},{8,5},{9,4},... | collective-permute-start | bytes 221192 | tf_op jit(solution)/shard_map/ppermute | solution.py:363
  12.8 9.7 %collective-permute-start.11 = (f32[144,128]{1,0:T(8,128)}, f32[144,128]{1,0:T(8,128)S(1)}, u32[]{:S(2)}, u32[]{:S(2)}) collective-permute-start(f32[144,128]{1,0:T(8,128)} %get-tuple-element.41), channel_id=1, source_target_pairs={{0,12},{1,13},{2,14},{3,15},{4,8},{5,9},{6,10},{7,11},{8,4},{9,5},... | collective-permute-start | bytes 221192 | tf_op jit(solution)/shard_map/ppermute | solution.py:363
  13.2 9.7 %collective-permute-start.12 = (f32[144,128]{1,0:T(8,128)}, f32[144,128]{1,0:T(8,128)S(1)}, u32[]{:S(2)}, u32[]{:S(2)}) collective-permute-start(f32[144,128]{1,0:T(8,128)} %get-tuple-element.42), channel_id=1, source_target_pairs={{0,3},{1,2},{2,1},{3,0},{4,7},{5,6},{6,5},{7,4},{8,11},{9,10},{10,... | collective-permute-start | bytes 221192 | tf_op jit(solution)/shard_map/ppermute | solution.py:363
  14.1 11.4 %collective-permute-start.13 = (f32[144,128]{1,0:T(8,128)}, f32[144,128]{1,0:T(8,128)S(1)}, u32[]{:S(2)}, u32[]{:S(2)}) collective-permute-start(f32[144,128]{1,0:T(8,128)} %get-tuple-element.43), channel_id=1, source_target_pairs={{0,2},{1,3},{2,0},{3,1},{4,6},{5,7},{6,4},{7,5},{8,10},{9,11},{10,... | collective-permute-start | bytes 221192 | tf_op jit(solution)/shard_map/ppermute | solution.py:363
  17.2 8.6 %collective-permute-start.14 = (f32[144,128]{1,0:T(8,128)}, f32[144,128]{1,0:T(8,128)S(1)}, u32[]{:S(2)}, u32[]{:S(2)}) collective-permute-start(f32[144,128]{1,0:T(8,128)} %get-tuple-element.44), channel_id=1, source_target_pairs={{0,1},{1,0},{2,3},{3,2},{4,5},{5,4},{6,7},{7,6},{8,9},{9,8},{10,11... | collective-permute-start | bytes 221192 | tf_op jit(solution)/shard_map/ppermute | solution.py:363
  17.3 15.5 %collective-permute-start.3 = (f32[144,128]{1,0:T(8,128)}, f32[144,128]{1,0:T(8,128)S(1)}, u32[]{:S(2)}, u32[]{:S(2)}) collective-permute-start(f32[144,128]{1,0:T(8,128)} %get-tuple-element.32), channel_id=1, source_target_pairs={{0,11},{1,10},{2,9},{3,8},{4,15},{5,14},{6,13},{7,12},{8,3},{9,2},... | collective-permute-start | bytes 221192 | tf_op jit(solution)/shard_map/ppermute | solution.py:363
  22.5 12.2 %collective-permute-start.4 = (f32[144,128]{1,0:T(8,128)}, f32[144,128]{1,0:T(8,128)S(1)}, u32[]{:S(2)}, u32[]{:S(2)}) collective-permute-start(f32[144,128]{1,0:T(8,128)} %get-tuple-element.33), channel_id=1, source_target_pairs={{0,7},{1,6},{2,5},{3,4},{4,3},{5,2},{6,1},{7,0},{8,15},{9,14},{10,... | collective-permute-start | bytes 221192 | tf_op jit(solution)/shard_map/ppermute | solution.py:363
  22.9 13.5 %collective-permute-start.5 = (f32[144,128]{1,0:T(8,128)}, f32[144,128]{1,0:T(8,128)S(1)}, u32[]{:S(2)}, u32[]{:S(2)}) collective-permute-start(f32[144,128]{1,0:T(8,128)} %get-tuple-element.34), channel_id=1, source_target_pairs={{0,6},{1,7},{2,4},{3,5},{4,2},{5,3},{6,0},{7,1},{8,14},{9,15},{10,... | collective-permute-start | bytes 221192 | tf_op jit(solution)/shard_map/ppermute | solution.py:363
  25.5 11.6 %collective-permute-start.6 = (f32[144,128]{1,0:T(8,128)}, f32[144,128]{1,0:T(8,128)S(1)}, u32[]{:S(2)}, u32[]{:S(2)}) collective-permute-start(f32[144,128]{1,0:T(8,128)} %get-tuple-element.35), channel_id=1, source_target_pairs={{0,5},{1,4},{2,7},{3,6},{4,1},{5,0},{6,3},{7,2},{8,13},{9,12},{10,... | collective-permute-start | bytes 221192 | tf_op jit(solution)/shard_map/ppermute | solution.py:363
  25.8 11.2 %collective-permute-start.7 = (f32[144,128]{1,0:T(8,128)}, f32[144,128]{1,0:T(8,128)S(1)}, u32[]{:S(2)}, u32[]{:S(2)}) collective-permute-start(f32[144,128]{1,0:T(8,128)} %get-tuple-element.36), channel_id=1, source_target_pairs={{0,4},{1,5},{2,6},{3,7},{4,0},{5,1},{6,2},{7,3},{8,12},{9,13},{10,... | collective-permute-start | bytes 221192 | tf_op jit(solution)/shard_map/ppermute | solution.py:363
  26.9 0.9 %copy-start = (f32[144,128]{1,0:T(8,128)S(1)}, f32[144,128]{1,0:T(8,128)}, u32[]{:S(2)}) copy-start(f32[144,128]{1,0:T(8,128)} %get-tuple-element.37.refs_0_) | copy-start | bytes 221188
  27.8 4.9 %copy-start.4 = (f32[144,128]{1,0:T(8,128)S(1)}, f32[144,128]{1,0:T(8,128)}, u32[]{:S(2)}) copy-start(f32[144,128]{1,0:T(8,128)} %get-tuple-element.29) | copy-start | bytes 221188
  27.8 6.9 %copy-start.3 = (f32[144,128]{1,0:T(8,128)S(1)}, f32[144,128]{1,0:T(8,128)}, u32[]{:S(2)}) copy-start(f32[144,128]{1,0:T(8,128)} %get-tuple-element.30) | copy-start | bytes 221188
  27.8 8.6 %copy-start.2 = (f32[144,128]{1,0:T(8,128)S(1)}, f32[144,128]{1,0:T(8,128)}, u32[]{:S(2)}) copy-start(f32[144,128]{1,0:T(8,128)} %get-tuple-element.31) | copy-start | bytes 221188
  32.7 11.3 %collective-permute-start = (f32[144,128]{1,0:T(8,128)S(1)}, f32[144,128]{1,0:T(8,128)S(1)}, u32[]{:S(2)}, u32[]{:S(2)}) collective-permute-start(f32[144,128]{1,0:T(8,128)S(1)} %copy-done.4), channel_id=1, source_target_pairs={{0,10},{1,11},{2,8},{3,9},{4,14},{5,15},{6,12},{7,13},{8,2},{9,3},... | collective-permute-start | bytes 221192 | tf_op jit(solution)/shard_map/ppermute | solution.py:363
  34.7 10.5 %collective-permute-start.1 = (f32[144,128]{1,0:T(8,128)S(1)}, f32[144,128]{1,0:T(8,128)S(1)}, u32[]{:S(2)}, u32[]{:S(2)}) collective-permute-start(f32[144,128]{1,0:T(8,128)S(1)} %copy-done.3), channel_id=1, source_target_pairs={{0,9},{1,8},{2,11},{3,10},{4,13},{5,12},{6,15},{7,14},{8,1},{9,0},... | collective-permute-start | bytes 221192 | tf_op jit(solution)/shard_map/ppermute | solution.py:363
  36.4 10.4 %collective-permute-start.2 = (f32[144,128]{1,0:T(8,128)S(1)}, f32[144,128]{1,0:T(8,128)S(1)}, u32[]{:S(2)}, u32[]{:S(2)}) collective-permute-start(f32[144,128]{1,0:T(8,128)S(1)} %copy-done.2), channel_id=1, source_target_pairs={{0,8},{1,9},{2,10},{3,11},{4,12},{5,13},{6,14},{7,15},{8,0},{9,1},... | collective-permute-start | bytes 221192 | tf_op jit(solution)/shard_map/ppermute | solution.py:363
  37.0 9.8 %copy-start.1 = (f32[20,128]{1,0:T(8,128)S(1)}, f32[20,128]{1,0:T(8,128)}, u32[]{:S(2)}) copy-start(f32[20,128]{1,0:T(8,128)} %get-tuple-element.49.refs_5_) | copy-start | bytes 30724
